TPU v7x, 16 devices: a whole 2x2x2 slice. The times are simulated.
16 devices in a mesh: model: 4 (over z, y), fsdp: 4 (over x, core).
Axes of the slice: x: 2, y: 2, z: 2, core: 2. Of those that a mesh axis runs over, the one named last changes fastest.
Arguments:
- tok_ids: int32 [4, 2048], P('fsdp')
- tok_labels: int32 [4, 2048], P('fsdp')
- emb_table: bfloat16 [50304, 768], P(('model', 'fsdp'))
- w_gate: bfloat16 [768, 3072], P('fsdp')
- w_up: bfloat16 [768, 3072], P('fsdp')
- w_down: bfloat16 [3072, 768], P('fsdp')
- gain_in: float32 [768], replicated
- gain_out: float32 [768], replicated
Outputs:
- output 1: float32 [], replicated
- output 2: float32 [50304, 768], P(('model', 'fsdp'))
- output 3: float32 [768, 3072], P('fsdp')
- output 4: float32 [768, 3072], P('fsdp')
- output 5: float32 [3072, 768], P('fsdp')
All inputs are finite; a program needn't handle non-finite values.
Results may differ from a plain program's by a relative error of at most 0.0100315.
Values are sent between devices in bfloat16 or wider.
A program may use at most 1 GiB of HBM per device.

v0:
```python
import jax
import jax.numpy as jnp
from jax import lax
from jax.sharding import PartitionSpec as P

EPS = 1e-6


def rms_scale(values, gain_vec):
    mean_sq = jnp.mean(values * values, axis=-1, keepdims=True)
    return values * lax.rsqrt(mean_sq + EPS) * gain_vec


def mlp_forward(x_emb, gain_in, w_gate, w_up, w_down):
    normed_in, norm_in_back = jax.vjp(lambda values: rms_scale(values, gain_in), x_emb)
    normed_bf = normed_in.astype(jnp.bfloat16)
    gate_f = jnp.dot(normed_bf, w_gate, preferred_element_type=jnp.float32).astype(jnp.bfloat16).astype(jnp.float32)
    up_f = jnp.dot(normed_bf, w_up, preferred_element_type=jnp.float32).astype(jnp.bfloat16).astype(jnp.float32)
    gate_sig = jax.nn.sigmoid(gate_f)
    silu_gate = gate_f * gate_sig
    act_bf = (silu_gate * up_f).astype(jnp.bfloat16)
    mlp_out = jnp.dot(act_bf, w_down, preferred_element_type=jnp.float32).astype(jnp.bfloat16)
    h_res = x_emb + mlp_out.astype(jnp.float32)
    return h_res, (norm_in_back, normed_bf, gate_f, up_f, gate_sig, silu_gate, act_bf)


def mlp_backward(d_hidden, saved, w_gate, w_up, w_down):
    norm_in_back, normed_bf, gate_f, up_f, gate_sig, silu_gate, act_bf = saved
    d_mlp = d_hidden.astype(jnp.bfloat16)
    d_act = jnp.einsum("td,fd->tf", d_mlp, w_down, preferred_element_type=jnp.float32)
    grad_down = jnp.einsum("tf,td->fd", act_bf, d_mlp, preferred_element_type=jnp.float32)
    d_gate = (d_act * up_f * (gate_sig * (1.0 + gate_f * (1.0 - gate_sig)))).astype(jnp.bfloat16)
    d_up = (d_act * silu_gate).astype(jnp.bfloat16)
    grad_gate = jnp.einsum("td,tf->df", normed_bf, d_gate, preferred_element_type=jnp.float32)
    grad_up = jnp.einsum("td,tf->df", normed_bf, d_up, preferred_element_type=jnp.float32)
    d_normed = jnp.einsum("tf,df->td", d_gate, w_gate, preferred_element_type=jnp.float32) + jnp.einsum("tf,df->td", d_up, w_up, preferred_element_type=jnp.float32)
    d_x = d_hidden + norm_in_back(d_normed)[0]
    return d_x, grad_gate, grad_up, grad_down


def solution(mesh):
    fsdp_size = mesh.shape["fsdp"]
    tok_spec = P("fsdp", None)
    row_spec = P(("model", "fsdp"), None)
    weight_spec = P("fsdp", None)

    def device_step(tok_ids, tok_labels, table_shard, gate_shard, up_shard, down_shard, gain_in, gain_out):
        local_count = tok_ids.shape[0] * tok_ids.shape[1]
        num_tokens = local_count * fsdp_size
        table_part = lax.all_gather(table_shard, "fsdp", axis=0, tiled=True)
        w_gate = lax.all_gather(gate_shard, "fsdp", axis=0, tiled=True)
        w_up = lax.all_gather(up_shard, "fsdp", axis=0, tiled=True)
        w_down = lax.all_gather(down_shard, "fsdp", axis=0, tiled=True)
        vocab_part = table_part.shape[0]
        vocab_start = lax.axis_index("model") * vocab_part
        local_ids = tok_ids.reshape(local_count) - vocab_start
        id_inside = (local_ids >= 0) & (local_ids < vocab_part)
        safe_ids = jnp.where(id_inside, local_ids, 0)
        emb_rows = jnp.where(id_inside[:, None], jnp.take(table_part, safe_ids, axis=0), 0)
        x_emb = lax.psum(emb_rows, "model").astype(jnp.float32)
        h_res, saved = mlp_forward(x_emb, gain_in, w_gate, w_up, w_down)
        hn_f, norm_out_back = jax.vjp(lambda values: rms_scale(values, gain_out), h_res)
        hn_bf = hn_f.astype(jnp.bfloat16)
        logits = jnp.einsum("td,vd->tv", hn_bf, table_part, preferred_element_type=jnp.float32)
        row_max = lax.pmax(jnp.max(logits, axis=-1), "model")
        exp_shift = jnp.exp(logits - row_max[:, None])
        local_labels = tok_labels.reshape(local_count) - vocab_start
        onehot = lax.broadcasted_iota(jnp.int32, logits.shape, 1) == local_labels[:, None]
        part_stats = jnp.stack([jnp.sum(exp_shift, axis=-1), jnp.sum(jnp.where(onehot, logits, 0.0), axis=-1)])
        tok_stats = lax.psum(part_stats, "model")
        sum_exp = tok_stats[0]
        tok_loss = row_max + jnp.log(sum_exp) - tok_stats[1]
        loss = lax.psum(jnp.sum(tok_loss), "fsdp") / num_tokens
        soft_probs = exp_shift / sum_exp[:, None]
        d_logits = (jnp.where(onehot, soft_probs - 1.0, soft_probs) / num_tokens).astype(jnp.bfloat16)
        d_head = jnp.einsum("tv,td->vd", d_logits, hn_bf, preferred_element_type=jnp.float32)
        d_hn = lax.psum(jnp.einsum("tv,vd->td", d_logits, table_part, preferred_element_type=jnp.float32), "model")
        d_hidden = norm_out_back(d_hn)[0]
        d_x, grad_gate, grad_up, grad_down = mlp_backward(d_hidden, saved, w_gate, w_up, w_down)
        d_in = jax.ops.segment_sum(jnp.where(id_inside[:, None], d_x, 0.0), safe_ids, num_segments=vocab_part)
        grad_table = lax.psum_scatter(d_head + d_in, "fsdp", scatter_dimension=0, tiled=True)
        grad_gate = lax.psum_scatter(grad_gate, "fsdp", scatter_dimension=0, tiled=True)
        grad_up = lax.psum_scatter(grad_up, "fsdp", scatter_dimension=0, tiled=True)
        grad_down = lax.psum_scatter(grad_down, "fsdp", scatter_dimension=0, tiled=True)
        return loss, grad_table, grad_gate, grad_up, grad_down

    return jax.shard_map(device_step, mesh=mesh, in_specs=(tok_spec, tok_spec, row_spec, weight_spec, weight_spec, weight_spec, P(), P()), out_specs=(P(), row_spec, weight_spec, weight_spec, weight_spec), check_vma=False)
```

profile of v0, /device:TPU:0, one launch (start us, length us, event | category | flops | bytes accessed | tf_op | source)
XLA Modules:
  0.0 1259.8 jit_solution(11694124990307840745)
XLA Ops:
  7.2 0.0 all-gather.5.cloned.1.call-start
  7.2 0.7 all-gather.5.cloned.1.call-update
  7.9 0.0 all-reduce.4.cloned.1.call-start
  8.0 1.3 compare_select_fusion
  9.3 124.5 %all-gather.5.cloned.1.call-done = bf16[12576,768]{1,0:T(8,128)(2,1)} async-done(((bf16[3144,768]{1,0:T(8,128)(2,1)}), bf16[12576,768]{1,0:T(8,128)(2,1)}) %all-gather.5.cloned.1.call-update) | async-done | bytes 19316752 | tf_op jit(solution)/shard_map/all_gather | solution.py:50
  133.8 19.0 %gather_fusion = bf16[2048,768]{1,0:T(8,128)(2,1)} fusion(bf16[12576,768]{1,0:T(8,128)(2,1)} %all-gather.5.cloned.1.call-done, s32[2048]{0:T(1024)S(1)} %broadcast_clamp_fusion), kind=kCustom, calls=%fused_computation | custom fusion | bytes 6299648 | tf_op jit(solution)/shard_map/jit(_take)/gather | solution.py:59
  152.8 3.2 copy.18
  156.0 2.0 select_select_fusion
  158.1 0.0 all-reduce.4.cloned.1.call-update
  158.1 0.0 all-gather.7.cloned.1.call-start
  158.1 0.7 all-gather.7.cloned.1.call-update
  158.8 0.0 all-gather.9.cloned.1.call-start
  158.9 0.5 all-gather.9.cloned.1.call-update
  159.4 0.0 all-gather.11.cloned.1.call-start
  159.4 0.5 all-gather.11.cloned.1.call-update
  160.0 0.4 all-reduce.6.cloned.1.call-start
  160.4 0.6 broadcast_subtract_fusion
  161.0 76.1 %all-reduce.4.cloned.1.call-done = bf16[2048,768]{0,1:T(8,128)(2,1)} async-done(((bf16[2048,768]{0,1:T(8,128)(2,1)}), bf16[2048,768]{0,1:T(8,128)(2,1)}) %all-reduce.4.cloned.1.call-update) | async-done | bytes 3145744 | tf_op jit(solution)/shard_map/psum | solution.py:60
  237.2 2.6 fusion.13
  239.7 0.6 copy-done.6
  240.3 33.9 %all-gather.7.cloned.1.call-done = bf16[768,3072]{1,0:T(8,128)(2,1)} async-done(((bf16[192,3072]{1,0:T(8,128)(2,1)}), bf16[768,3072]{1,0:T(8,128)(2,1)}) %all-gather.7.cloned.1.call-update) | async-done | bytes 4718608 | tf_op jit(solution)/shard_map/all_gather | solution.py:51
  274.2 16.1 %convolution_convert_fusion.1 = bf16[2048,3072]{1,0:T(8,128)(2,1)} fusion(bf16[768,3072]{1,0:T(8,128)(2,1)} %all-gather.7.cloned.1.call-done, bf16[2048,768]{0,1:T(8,128)(2,1)} %all-reduce.4.cloned.1.call-done, f32[768]{0:T(1024)S(1)} %copy-done.23, f32[2048]{0:T(1024)S(1)} %fusion.21), kind=kOutput, calls=%fused_computation.29 | convolution fusion | flops 9676259328 | bytes 20458496 | tf_op jit(solution)/shard_map/dot_general | solution.py:17
  290.3 20.8 %all-gather.9.cloned.1.call-done = bf16[768,3072]{1,0:T(8,128)(2,1)} async-done(((bf16[192,3072]{1,0:T(8,128)(2,1)}), bf16[768,3072]{1,0:T(8,128)(2,1)}) %all-gather.9.cloned.1.call-update) | async-done | bytes 4718608 | tf_op jit(solution)/shard_map/all_gather | solution.py:52
  311.1 22.4 %fusion.3 = (bf16[2048,3072]{1,0:T(8,128)(2,1)}, bf16[2048,3072]{1,0:T(8,128)(2,1)}) fusion(bf16[2048,3072]{1,0:T(8,128)(2,1)} %convolution_convert_fusion.1, bf16[768,3072]{1,0:T(8,128)(2,1)} %all-gather.9.cloned.1.call-done, bf16[2048,768]{0,1:T(8,128)(2,1)S(1)} %copy-done, f32[768]{0:T(1024)S(1)} %copy-done.23, f32[2048]{0:T(1024)S(1)} %fusion.21), kind=kOutput, calls=%fused_computation.14 | convolution fusion | flops 9726590976 | bytes 45624320 | tf_op jit(solution)/shard_map/dot_general | solution.py:18
  333.5 14.4 %all-gather.11.cloned.1.call-done = bf16[3072,768]{1,0:T(8,128)(2,1)} async-done(((bf16[768,768]{1,0:T(8,128)(2,1)}), bf16[3072,768]{1,0:T(8,128)(2,1)}) %all-gather.11.cloned.1.call-update) | async-done | bytes 4718608 | tf_op jit(solution)/shard_map/all_gather | solution.py:53
  347.9 26.1 %multiply_reduce_fusion.1 = (f32[2048]{0:T(1024)S(1)}, bf16[2048,768]{0,1:T(8,128)(2,1)}) fusion(bf16[2048,768]{0,1:T(8,128)(2,1)S(1)} %copy-done, bf16[2048,3072]{1,0:T(8,128)(2,1)} %get-tuple-element.16, bf16[3072,768]{1,0:T(8,128)(2,1)} %all-gather.11.cloned.1.call-done), kind=kOutput, calls=%fused_computation.41 | convolution fusion | flops 9673111552 | bytes 23601152 | tf_op jit(solution)/shard_map/dot_general | solution.py:22
  374.1 0.6 copy-done.14
  374.6 52.0 %fusion.32 = (f32[2048]{0:T(1024)S(1)}, f32[2048,12576]{0,1:T(8,128)}) fusion(bf16[12576,768]{1,0:T(8,128)(2,1)} %all-gather.5.cloned.1.call-done, bf16[2048,768]{0,1:T(8,128)(2,1)} %get-tuple-element.19, bf16[2048,768]{0,1:T(8,128)(2,1)S(1)} %copy-done, f32[768]{0:T(1024)S(1)} %copy-done.20, f32[2048]{0:T(1024)S(1)} %fusion.22), kind=kOutput, calls=%fused_computation.69 | convolution fusion | flops 39595868160 | bytes 128650240 | tf_op jit(solution)/shard_map/td,vd->tv/dot_general | solution.py:64
  426.6 10.0 pmax.7
  436.6 32.1 %fusion.2 = (f32[2048]{0:T(1024)S(1)}, f32[2048]{0:T(1024)S(1)}) fusion(f32[2048,12576]{0,1:T(8,128)} %get-tuple-element.21, f32[2048]{0:T(1024)S(1)} %pmax.7, s32[2048]{0:T(1024)S(1)} %bitcast.31), kind=kLoop, calls=%fused_computation.8 | loop fusion | flops 128774144 | bytes 103055360 | tf_op jit(solution)/shard_map/reduce_sum | solution.py:69
  468.8 14.4 %psum.29 = f32[2,2048]{1,0:T(2,128)S(1)} all-reduce(f32[2,2048]{1,0:T(2,128)S(1)} %pad_maximum_fusion), channel_id=1, replica_groups=mesh['model'=4,'fsdp'=4] {'model'}, use_global_device_ids=true, to_apply=%region_7.8 | all-reduce | flops 4096 | bytes 32768 | tf_op jit(solution)/shard_map/psum | solution.py:70
  483.1 0.6 fusion.31
  483.7 50.2 %fusion.1 = bf16[2048,12576]{0,1:T(8,128)(2,1)} fusion(f32[2048,12576]{0,1:T(8,128)} %get-tuple-element.21, f32[2048]{0:T(1024)S(1)} %bitcast.33, s32[2048]{0:T(1024)S(1)} %bitcast.32, f32[2048]{0:T(1024)S(1)} %pmax.7), kind=kLoop, calls=%fused_computation.4 | loop fusion | flops 180289536 | bytes 154558464 | tf_op jit(solution)/shard_map/convert_element_type | solution.py:75
  534.0 50.0 %fusion.33 = f32[2048,768]{0,1:T(8,128)} fusion(bf16[2048,12576]{0,1:T(8,128)(2,1)} %fusion.1, bf16[12576,768]{1,0:T(8,128)(2,1)} %all-gather.5.cloned.1.call-done), kind=kOutput, calls=%fused_computation.70 | convolution fusion | flops 39560675328 | bytes 77119488 | tf_op jit(solution)/shard_map/tv,vd->td/dot_general | solution.py:77
  584.0 0.0 all-reduce.6.cloned.1.call-update
  584.1 0.4 reduce-scatter.7.cloned.1.call-start
  584.5 128.9 %all-reduce.6.cloned.1.call-done = f32[2048,768]{0,1:T(8,128)} async-done(((f32[2048,768]{0,1:T(8,128)}), f32[2048,768]{0,1:T(8,128)}) %all-reduce.6.cloned.1.call-update) | async-done | bytes 6291472 | tf_op jit(solution)/shard_map/psum | solution.py:77
  713.4 5.5 multiply_reduce_fusion
  719.0 29.2 %multiply_convert_fusion = (bf16[2048,3072]{1,0:T(8,128)(2,1)}, bf16[2048,3072]{1,0:T(8,128)(2,1)}) fusion(bf16[2048,3072]{1,0:T(8,128)(2,1)} %convolution_convert_fusion.1, bf16[2048,3072]{1,0:T(8,128)(2,1)} %get-tuple-element.17, bf16[3072,768]{1,0:T(8,128)(2,1)} %all-gather.11.cloned.1.call-done, f32[2048]{0:T(1024)S(1)} %multiply_multiply_fusion.1, ...), kind=kOutput, calls=%fused_computation.22 | convolution fusion | flops 9772204032 | bytes 67652608 | tf_op jit(solution)/shard_map/td,fd->tf/dot_general | solution.py:30
  748.2 15.1 %fusion.27 = f32[768,3072]{1,0:T(8,128)} fusion(bf16[2048,3072]{1,0:T(8,128)(2,1)} %get-tuple-element.11, bf16[2048,768]{0,1:T(8,128)(2,1)S(1)} %copy-done.1, f32[768]{0:T(1024)S(1)} %copy-done.24, f32[2048]{0:T(1024)S(1)} %copy-done.11), kind=kOutput, calls=%fused_computation.67 | convolution fusion | flops 9669967872 | bytes 25177088 | tf_op jit(solution)/shard_map/td,tf->df/dot_general | solution.py:34
  763.3 0.0 reduce-scatter.7.cloned.1.call-update
  763.3 0.2 reduce-scatter.9.cloned.1.call-start
  763.5 15.2 %fusion.25 = f32[768,3072]{1,0:T(8,128)} fusion(bf16[2048,3072]{1,0:T(8,128)(2,1)} %get-tuple-element.10, bf16[2048,768]{0,1:T(8,128)(2,1)S(1)} %copy-done.1, f32[768]{0:T(1024)S(1)} %copy-done.24, f32[2048]{0:T(1024)S(1)} %copy-done.11), kind=kOutput, calls=%fused_computation.66 | convolution fusion | flops 9669967872 | bytes 25177088 | tf_op jit(solution)/shard_map/td,tf->df/dot_general | solution.py:35
  778.7 0.0 reduce-scatter.9.cloned.1.call-update
  778.7 0.0 reduce-scatter.11.cloned.1.call-start
  778.7 18.6 %fusion.17 = f32[3072,768]{1,0:T(8,128)} fusion(bf16[2048,3072]{1,0:T(8,128)(2,1)} %get-tuple-element.16, f32[2048,768]{0,1:T(8,128)} %all-reduce.6.cloned.1.call-done, bf16[2048,768]{0,1:T(8,128)(2,1)} %get-tuple-element.19, bf16[2048,768]{0,1:T(8,128)(2,1)S(1)} %copy-done.1, f32[2048]{0:T(1024)S(1)} %multiply_multiply_fusion.1, f32[768]{0:T(1024)S(1)} %copy-done.21, ...), kind=kOutput, calls=%fused_computation.44 | convolution fusion | flops 9677832192 | bytes 34622464 | tf_op jit(solution)/shard_map/tf,td->fd/dot_general | solution.py:31
  797.3 0.0 reduce-scatter.11.cloned.1.call-update
  797.3 0.3 reduce-scatter.13.cloned.1.call-start
  797.6 50.0 %fusion.23 = f32[12576,768]{1,0:T(8,128)} fusion(bf16[2048,12576]{0,1:T(8,128)(2,1)} %fusion.1, bf16[2048,768]{0,1:T(8,128)(2,1)} %get-tuple-element.19, bf16[2048,768]{0,1:T(8,128)(2,1)S(1)} %copy-done.1, f32[768]{0:T(1024)S(1)} %copy-done.21, f32[2048]{0:T(1024)S(1)} %copy-done.13), kind=kOutput, calls=%fused_computation.64 | convolution fusion | flops 39570112512 | bytes 96447488 | tf_op jit(solution)/shard_map/tv,td->vd/dot_general | solution.py:76
  847.6 16.1 %fusion.34 = f32[2048,768]{0,1:T(8,128)} fusion(bf16[2048,3072]{1,0:T(8,128)(2,1)} %get-tuple-element.11, bf16[768,3072]{1,0:T(8,128)(2,1)} %all-gather.7.cloned.1.call-done), kind=kOutput, calls=%fused_computation.71 | convolution fusion | flops 9663676416 | bytes 23592960 | tf_op jit(solution)/shard_map/tf,df->td/dot_general | solution.py:36
  863.7 15.9 %fusion.16 = (f32[2048]{0:T(1024)S(1)}, f32[2048,768]{0,1:T(8,128)S(1)}) fusion(bf16[2048,768]{0,1:T(8,128)(2,1)S(1)} %copy-done.1, f32[768]{0:T(1024)S(1)} %copy-done.24, f32[2048,768]{0,1:T(8,128)} %fusion.34, bf16[2048,3072]{1,0:T(8,128)(2,1)} %get-tuple-element.10, bf16[768,3072]{1,0:T(8,128)(2,1)} %all-gather.9.cloned.1.call-done), kind=kOutput, calls=%fused_computation.37 | convolution fusion | flops 9671538688 | bytes 33041408 | tf_op jit(solution)/shard_map/tf,df->td/dot_general | solution.py:36
  879.7 5.1 fusion.12
  884.8 6.6 copy.20
  891.4 39.2 %scatter_fusion = f32[12576,768]{1,0:T(8,128)} fusion(f32[12576,768]{1,0:T(8,128)} %fusion.23, s32[2048]{0:T(1024)S(1)} %bitcast.40, f32[2048,768]{1,0:T(8,128)} %copy.20), kind=kCustom, calls=%fused_computation.1 | custom fusion | flops 1572864 | bytes 18882560 | tf_op jit(solution)/shard_map/scatter-add | solution.py:80
  930.6 0.0 reduce-scatter.13.cloned.1.call-update
  930.6 0.7 copy-done.4
  931.3 0.0 copy-done.9
  931.3 0.0 copy-done.16
  931.3 0.6 subtract_reduce_fusion
  931.9 7.0 psum.30
  939.5 0.0 reduce-scatter.7.cloned.1.call-done
  939.6 0.0 reduce-scatter.9.cloned.1.call-done
  939.6 50.2 %reduce-scatter.11.cloned.1.call-done = f32[768,768]{1,0:T(8,128)} async-done(((f32[3072,768]{1,0:T(8,128)}), f32[768,768]{1,0:T(8,128)}) %reduce-scatter.11.cloned.1.call-update) | async-done | bytes 2359312 | tf_op jit(solution)/shard_map/reduce_scatter | solution.py:84
  989.8 261.7 %reduce-scatter.13.cloned.1.call-done = f32[3144,768]{1,0:T(8,128)} async-done(((f32[12576,768]{1,0:T(8,128)}), f32[3144,768]{1,0:T(8,128)}) %reduce-scatter.13.cloned.1.call-update) | async-done | bytes 9658384
  (57 shorter events, 0.2 us)
Async XLA Ops:
  7.2 126.6 %all-gather.5.cloned.1.call-start = ((), (), s32[]{:S(2)}) async-start(), calls=%async_computation.4 | async-start | bytes 24145920 | tf_op jit(solution)/shard_map/all_gather | solution.py:50
  7.9 229.3 %all-reduce.4.cloned.1.call-start = ((), (), s32[]{:S(2)}) async-start(), calls=%async_computation.5 | async-start | bytes 6291456 | tf_op jit(solution)/shard_map/psum | solution.py:60
  9.3 146.8 %copy-start.18 = (pred[2048]{0:T(1024)(128)(4,1)}, pred[2048]{0:T(1024)(128)(4,1)S(1)}, u32[]{:S(2)}) copy-start(pred[2048]{0:T(1024)(128)(4,1)S(1)} %get-tuple-element.14) | copy-start | bytes 6148
  156.0 4.4 copy-start.22
  158.1 116.1 %copy-start.23 = (f32[768]{0:T(1024)S(1)}, f32[768]{0:T(1024)}, u32[]{:S(2)}) copy-start(f32[768]{0:T(1024)} %param.14) | copy-start | bytes 9220
  158.1 116.1 %all-gather.7.cloned.1.call-start = ((), (), s32[]{:S(2)}) async-start(), calls=%async_computation.6 | async-start | bytes 5898240 | tf_op jit(solution)/shard_map/all_gather | solution.py:51
  158.8 152.2 %all-gather.9.cloned.1.call-start = ((), (), s32[]{:S(2)}) async-start(), calls=%async_computation.7 | async-start | bytes 5898240 | tf_op jit(solution)/shard_map/all_gather | solution.py:52
  159.4 188.5 %all-gather.11.cloned.1.call-start = ((), (), s32[]{:S(2)}) async-start(), calls=%async_computation.8 | async-start | bytes 5898240 | tf_op jit(solution)/shard_map/all_gather | solution.py:53
  160.0 553.5 %all-reduce.6.cloned.1.call-start = ((), (), s32[]{:S(2)}) async-start(), calls=%async_computation.9 | async-start | bytes 12582912 | tf_op jit(solution)/shard_map/psum | solution.py:77
  239.7 0.6 copy-start.6
  240.3 70.7 %copy-start.10 = (f32[2048]{0:T(1024)}, f32[2048]{0:T(1024)S(1)}, u32[]{:S(2)}) copy-start(f32[2048]{0:T(1024)S(1)} %fusion.21) | copy-start | bytes 24580
  240.3 70.7 %copy-start = (bf16[2048,768]{0,1:T(8,128)(2,1)S(1)}, bf16[2048,768]{0,1:T(8,128)(2,1)}, u32[]{:S(2)}) copy-start(bf16[2048,768]{0,1:T(8,128)(2,1)} %all-reduce.4.cloned.1.call-done) | copy-start | bytes 9437188
  347.9 26.7 %copy-start.20 = (f32[768]{0:T(1024)S(1)}, f32[768]{0:T(1024)}, u32[]{:S(2)}) copy-start(f32[768]{0:T(1024)} %param.15) | copy-start | bytes 9220
  374.0 0.6 copy-start.14
  374.6 52.0 %copy-start.12 = (f32[2048]{0:T(1024)}, f32[2048]{0:T(1024)S(1)}, u32[]{:S(2)}) copy-start(f32[2048]{0:T(1024)S(1)} %fusion.22) | copy-start | bytes 24580
  374.6 62.0 %copy-start.5 = (s32[1,2048]{1,0:T(1,128)S(1)}, s32[1,2048]{1,0:T(1,128)}, u32[]{:S(2)}) copy-start(s32[1,2048]{1,0:T(1,128)} %broadcast_subtract_fusion) | copy-start | bytes 24580
  436.6 47.1 %copy-start.3 = (f32[2048]{0:T(1024)}, f32[2048]{0:T(1024)S(1)}, u32[]{:S(2)}) copy-start(f32[2048]{0:T(1024)S(1)} %pmax.7) | copy-start | bytes 24580
  483.7 50.3 %copy-start.8 = (f32[1,2048]{1,0:T(1,128)}, f32[1,2048]{1,0:T(1,128)S(1)}, u32[]{:S(2)}) copy-start(f32[1,2048]{1,0:T(1,128)S(1)} %get-tuple-element.12) | copy-start | bytes 24580
  584.0 129.4 %copy-start.1 = (bf16[2048,768]{0,1:T(8,128)(2,1)S(1)}, bf16[2048,768]{0,1:T(8,128)(2,1)}, u32[]{:S(2)}) copy-start(bf16[2048,768]{0,1:T(8,128)(2,1)} %all-reduce.4.cloned.1.call-done) | copy-start | bytes 9437188
  584.0 129.4 %copy-start.21 = (f32[768]{0:T(1024)S(1)}, f32[768]{0:T(1024)}, u32[]{:S(2)}) copy-start(f32[768]{0:T(1024)} %param.15) | copy-start | bytes 9220
  584.0 134.9 %copy-start.15 = (f32[2048]{0:T(1024)S(1)}, f32[2048]{0:T(1024)}, u32[]{:S(2)}) copy-start(f32[2048]{0:T(1024)} %copy-done.14) | copy-start | bytes 24580
  584.1 134.9 %copy-start.13 = (f32[2048]{0:T(1024)S(1)}, f32[2048]{0:T(1024)}, u32[]{:S(2)}) copy-start(f32[2048]{0:T(1024)} %copy-done.12) | copy-start | bytes 24580
  584.1 355.5 %reduce-scatter.7.cloned.1.call-start = ((), (), s32[]{:S(2)}) async-start(), calls=%async_computation.10 | async-start | bytes 11796480 | tf_op jit(solution)/shard_map/reduce_scatter | solution.py:82
  719.0 29.2 %copy-start.11 = (f32[2048]{0:T(1024)S(1)}, f32[2048]{0:T(1024)}, u32[]{:S(2)}) copy-start(f32[2048]{0:T(1024)} %copy-done.10) | copy-start | bytes 24580
  719.0 29.2 %copy-start.24 = (f32[768]{0:T(1024)S(1)}, f32[768]{0:T(1024)}, u32[]{:S(2)}) copy-start(f32[768]{0:T(1024)} %param.14) | copy-start | bytes 9220
  763.3 176.3 %reduce-scatter.9.cloned.1.call-start = ((), (), s32[]{:S(2)}) async-start(), calls=%async_computation.11 | async-start | bytes 11796480 | tf_op jit(solution)/shard_map/reduce_scatter | solution.py:83
  778.7 211.1 %reduce-scatter.11.cloned.1.call-start = ((), (), s32[]{:S(2)}) async-start(), calls=%async_computation.12 | async-start | bytes 11796480 | tf_op jit(solution)/shard_map/reduce_scatter | solution.py:84
  797.3 454.2 %reduce-scatter.13.cloned.1.call-start = ((), (), s32[]{:S(2)}) async-start(), calls=%async_computation.13 | async-start | bytes 48291840
  847.6 32.0 %slice-start = ((s8[6291456]{0:T(1024)(128)(4,1)}), s8[4194304]{0:T(1024)(128)(4,1)S(1)}, s32[]{:S(2)}) async-start(s8[6291456]{0:T(1024)(128)(4,1)} %bitcast.29), calls=%async_computation.14 | async-start | bytes 8388608
  863.7 15.9 %copy-start.7 = (f32[2048]{0:T(1024)S(1)}, f32[2048]{0:T(1024)}, u32[]{:S(2)}) copy-start(f32[2048]{0:T(1024)} %copy-done.6) | copy-start | bytes 24580
  863.7 15.9 %slice-start.1 = ((s8[6291456]{0:T(1024)(128)(4,1)}), s8[2097152]{0:T(1024)(128)(4,1)S(1)}, s32[]{:S(2)}) async-start(s8[6291456]{0:T(1024)(128)(4,1)} %bitcast.29), calls=%async_computation.15 | async-start | bytes 4194304
  863.7 15.9 %copy-start.2 = (bf16[2048,768]{0,1:T(8,128)(2,1)S(1)}, bf16[2048,768]{0,1:T(8,128)(2,1)}, u32[]{:S(2)}) copy-start(bf16[2048,768]{0,1:T(8,128)(2,1)} %get-tuple-element.19) | copy-start | bytes 9437188
  863.7 15.9 %copy-start.19 = (pred[2048]{0:T(1024)(128)(4,1)S(1)}, pred[2048]{0:T(1024)(128)(4,1)}, u32[]{:S(2)}) copy-start(pred[2048]{0:T(1024)(128)(4,1)} %copy-done.18) | copy-start | bytes 6148
  884.8 6.6 copy-start.17
  930.6 0.7 copy-start.4
  930.6 0.7 copy-start.9
  930.6 0.7 copy-start.16
Sparse Core Ops, SparseCore 0:
  9.5 124.2 all-gather.4
  158.2 78.9 all-reduce.3
  238.7 35.4 all-gather.6
  275.6 35.4 all-gather.8
  312.4 35.4 all-gather.10
  584.2 129.2 all-reduce.5
  763.4 73.3 reduce-scatter.6
  839.9 73.3 reduce-scatter.8
  916.4 73.3 reduce-scatter.10
  992.9 258.6 reduce-scatter.12
where the time goes:
time: 1260 us
  waiting for transfers between devices  713 us (57%)
  matrix products  327 us (26%)
  other arithmetic  139 us (11%)
  local copies, waits for them, and re-layouts  31.4 us (2%)
  blocking collectives  31.3 us (2%)
  between operations  16.5 us (1%)
    unnamed x11, waiting for transfers between devices  264 us
    psum x1, waiting for transfers between devices, device_step(): lax.psum(jnp.einsum('tv,vd->td', d_logits, table_part, preferred_element_...  129 us
    all_gather x1, waiting for transfers between devices, device_step(): table_part = lax.all_gather(table_shard, 'fsdp', axis=0, tiled=True)  124 us
    psum x1, waiting for transfers between devices, device_step(): x_emb = lax.psum(emb_rows, 'model').astype(jnp.float32)  76.1 us
    dot_general x1, matrix products, device_step(): jnp.einsum('td,vd->tv', hn_bf, table_part, preferred_element_type=jnp.flo...  52 us
    convert_element_type x1, other arithmetic, device_step(): (jnp.where(onehot, soft_probs - 1.0, soft_probs) / num_tokens).astype(jnp...  50.2 us
    reduce_scatter x1, waiting for transfers between devices, device_step(): lax.psum_scatter(grad_down, 'fsdp', scatter_dimension=0, tiled=True)  50.2 us
    dot_general x1, matrix products, device_step(): jnp.einsum('tv,vd->td', d_logits, table_part, preferred_element_type=jnp....  50 us
  transfers between devices with their start and end apart: 10, of which 8 were waited for; matrix products, arithmetic and copies ran while one was open for 17% of the time, Pallas kernels for 0%

commit v1 on v0

v1 whole, which is shorter than its diff:
```python
import functools

import jax
import jax.numpy as jnp
from jax import lax
from jax.experimental import pallas as pl
from jax.experimental.pallas import tpu as pltpu
from jax.sharding import PartitionSpec as P

EPS = 1e-6
MESH = pl.DeviceIdType.MESH
AXES = ("model", "fsdp")
BF = jnp.bfloat16
F32 = jnp.float32
ROUND_ROWS = 64
VMEM_LIMIT = 64 * 1024 * 1024 - 128 * 1024


def rms_scale(values, gain_vec):
    mean_sq = jnp.mean(values * values, axis=-1, keepdims=True)
    return values * lax.rsqrt(mean_sq + EPS) * gain_vec


def my_place():
    m = lax.axis_index("model")
    f = lax.axis_index("fsdp")
    return (f // 2, m % 2, m // 2, f % 2)


def flipped(place, bits, core=False):
    x, y, z, c = place
    if bits & 1:
        x = 1 - x
    if bits & 2:
        y = 1 - y
    if bits & 4:
        z = 1 - z
    if core:
        c = 1 - c
    return (x, y, z, c)


def mesh_id(place):
    x, y, z, c = place
    return (2 * z + y, 2 * x + c)


def greet(place, bit_list, core):
    barrier = pltpu.get_barrier_semaphore()
    peers = [flipped(place, b) for b in bit_list] + ([flipped(place, 0, True)] if core else [])
    for peer in peers:
        pl.semaphore_signal(barrier, inc=1, device_id=mesh_id(peer), device_id_type=MESH)
    pl.semaphore_wait(barrier, len(peers))


ORDERS = ((1, 2, 4), (2, 4, 1), (4, 1, 2))


def subsets(bits):
    out = [0]
    for b in bits:
        out = out + [o | b for o in out]
    return out


def gather_kernel(parts, rows, in_ref, out_ref, local_sem, send_sem, recv_sem, core_send, core_recv):
    me = my_place()
    greet(me, (1, 2, 4), True)

    def block_of(place):
        m, f = mesh_id(place)
        return (m * 4 + f) * rows

    def out_part(place, color):
        lo, count = parts[color]
        return out_ref.at[pl.ds(pl.multiple_of(block_of(place) + lo, 8), count)]

    local = pltpu.make_async_copy(in_ref, out_ref.at[pl.ds(pl.multiple_of(block_of(me), 8), rows)], local_sem)
    local.start()
    sends = []

    def slot(color, stage, index):
        return color * 8 + (1 << stage) + index

    def chip_send(color, stage, index, bits):
        lo, count = parts[color]
        src = in_ref.at[pl.ds(lo, count)] if bits == 0 else out_part(flipped(me, bits), color)
        k = slot(color, stage, index)
        cp = pltpu.make_async_remote_copy(
            src_ref=src, dst_ref=out_part(flipped(me, bits), color),
            send_sem=send_sem.at[k], recv_sem=recv_sem.at[k],
            device_id=mesh_id(flipped(me, ORDERS[color][stage])), device_id_type=MESH)
        cp.start()
        sends.append(cp)

    def core_copy(color, bits, k):
        lo, count = parts[color]
        src = in_ref.at[pl.ds(lo, count)] if bits == 0 else out_part(flipped(me, bits), color)
        cp = pltpu.make_async_remote_copy(
            src_ref=src, dst_ref=out_part(flipped(me, bits), color),
            send_sem=core_send.at[k], recv_sem=core_recv.at[k],
            device_id=mesh_id(flipped(me, 0, True)), device_id_type=MESH)
        cp.start()
        sends.append(cp)

    for stage in range(3):
        for color in range(3):
            chip_send(color, stage, 0, 0)
    for color in range(3):
        core_copy(color, 0, color * 8)
    for stage in range(3):
        for index in range(1 << stage):
            for color in range(3):
                order = ORDERS[color]
                held = subsets(order[:stage])[index]
                bits = held | order[stage]
                k = slot(color, stage, index)
                pltpu.make_async_remote_copy(
                    src_ref=out_part(flipped(me, bits), color), dst_ref=out_part(flipped(me, bits), color),
                    send_sem=send_sem.at[k], recv_sem=recv_sem.at[k],
                    device_id=mesh_id(flipped(me, order[stage])), device_id_type=MESH).wait_recv()
                for later in range(stage + 1, 3):
                    chip_send(color, later, subsets(order[:later]).index(bits), bits)
                core_copy(color, bits, k)
    for color in range(3):
        for bits in range(8):
            order = ORDERS[color]
            if bits == 0:
                k = color * 8
            else:
                stage = max(s for s in range(3) if bits & order[s])
                k = slot(color, stage, subsets(order[:stage]).index(bits & ~order[stage]))
            dst = out_part(flipped(me, bits, True), color)
            pltpu.make_async_remote_copy(
                src_ref=dst, dst_ref=dst, send_sem=core_send.at[k], recv_sem=core_recv.at[k],
                device_id=mesh_id(flipped(me, 0, True)), device_id_type=MESH).wait_recv()
    for cp in sends:
        cp.wait_send()
    local.wait()


def gather_all(values, parts, collective_id):
    rows, width = values.shape
    any_spec = pl.BlockSpec(memory_space=pl.ANY)
    return pl.pallas_call(
        functools.partial(gather_kernel, parts, rows),
        out_shape=jax.ShapeDtypeStruct((16 * rows, width), values.dtype),
        in_specs=[any_spec], out_specs=any_spec,
        scratch_shapes=[pltpu.SemaphoreType.DMA, pltpu.SemaphoreType.DMA((24,)), pltpu.SemaphoreType.DMA((24,)),
                        pltpu.SemaphoreType.DMA((24,)), pltpu.SemaphoreType.DMA((24,))],
        compiler_params=pltpu.CompilerParams(collective_id=collective_id, has_side_effects=True),
        name=f"gather_all_{collective_id}",
    )(values)


CHUNK = 8


def add_rows(dst, slot_a, src, slot_b, rows):
    def body(i, carry):
        at = pl.ds(pl.multiple_of(i * CHUNK, CHUNK), CHUNK)
        dst[slot_a, at, :] = dst[slot_a, at, :] + src[slot_b, at, :]
        return carry

    lax.fori_loop(0, rows // CHUNK, body, 0)


BLOCK_ORDER = (7, 6, 5, 3, 4, 2, 1, 0)


def reduce_kernel(views, spread, *refs):
    n_in = max(v[0] for v in views) + 1
    ins = refs[:n_in]
    outs = refs[n_in:n_in + 3]
    accs = refs[n_in + 3:n_in + 6]
    pairs = refs[n_in + 6:n_in + 9]
    boxes = refs[n_in + 9:n_in + 12]
    load_sem, core_send, core_recv, send_sem, recv_sem, out_sem, sp_send, sp_recv = refs[n_in + 12:]
    me = my_place()
    greet(me, (1, 2, 4), True)
    sends = []
    loads = {}

    def source(color, place):
        which, rows, start = views[color]
        m, f = mesh_id(place)
        return ins[which].at[pl.ds(pl.multiple_of(start(m, f), 8), rows)]

    def core_copy(color, bits):
        k = color * 8 + bits
        return pltpu.make_async_remote_copy(
            src_ref=source(color, flipped(me, bits, True)), dst_ref=pairs[color].at[bits],
            send_sem=core_send.at[k], recv_sem=core_recv.at[k],
            device_id=mesh_id(flipped(me, 0, True)), device_id_type=MESH)

    for bits in BLOCK_ORDER:
        for color in range(3):
            cp = core_copy(color, bits)
            cp.start()
            sends.append(cp)
            ld = pltpu.make_async_copy(source(color, flipped(me, bits)), accs[color].at[bits], load_sem.at[color * 8 + bits])
            ld.start()
            loads[color, bits] = ld

    def stage_of(color, bits):
        order = ORDERS[color]
        for s in range(3):
            if bits & order[s]:
                return s
        return 3

    def box_slot(color, stage, bits):
        order = ORDERS[color]
        rest = subsets(order[stage + 1:])
        return (0, 4, 6)[stage] + rest.index(bits)

    def chip_copy(color, stage, bits):
        order = ORDERS[color]
        slot = box_slot(color, stage, bits & ~order[stage])
        k = color * 8 + slot
        return pltpu.make_async_remote_copy(
            src_ref=accs[color].at[bits], dst_ref=boxes[color].at[slot],
            send_sem=send_sem.at[k], recv_sem=recv_sem.at[k],
            device_id=mesh_id(flipped(me, order[stage])), device_id_type=MESH)

    for bits in BLOCK_ORDER:
        for color in range(3):
            loads[color, bits].wait()
            core_copy(color, bits).wait_recv()
            add_rows(accs[color], bits, pairs[color], bits, views[color][1])
            if stage_of(color, bits) == 0:
                cp = chip_copy(color, 0, bits)
                cp.start()
                sends.append(cp)
    for stage in range(3):
        for color in range(3):
            order = ORDERS[color]
            arriving = subsets(order[stage + 1:])
            for bits in sorted(arriving, key=lambda b: stage_of(color, b)):
                slot = box_slot(color, stage, bits)
                chip_copy(color, stage, bits | order[stage]).wait_recv()
                add_rows(accs[color], bits, boxes[color], slot, views[color][1])
                if stage_of(color, bits) == stage + 1 and stage < 2:
                    cp = chip_copy(color, stage + 1, bits)
                    cp.start()
                    sends.append(cp)
    locals_ = []
    if spread is None:
        for color in range(3):
            cp = pltpu.make_async_copy(accs[color].at[0], outs[color], out_sem.at[color])
            cp.start()
            locals_.append(cp)
    else:
        halves = ((2, 4), (4, 2))

        def target(color, place, half):
            rows = views[color][1]
            m, f = mesh_id(place)
            return outs[color].at[pl.ds(pl.multiple_of(m * rows + half * (rows // 2), 8), rows // 2)]

        def spread_copy(color, half, step, bits):
            rows = views[color][1]
            first, second = halves[half]
            src = accs[color].at[0, pl.ds(half * (rows // 2), rows // 2)] if bits == 0 else target(color, flipped(me, bits), half)
            k = (color * 2 + half) * 3 + step
            return pltpu.make_async_remote_copy(
                src_ref=src, dst_ref=target(color, flipped(me, bits), half),
                send_sem=sp_send.at[k], recv_sem=sp_recv.at[k],
                device_id=mesh_id(flipped(me, first if step == 0 else second)), device_id_type=MESH)

        for color in range(3):
            rows = views[color][1]
            m, f = mesh_id(me)
            cp = pltpu.make_async_copy(accs[color].at[0], outs[color].at[pl.ds(pl.multiple_of(m * rows, 8), rows)], out_sem.at[color])
            cp.start()
            locals_.append(cp)
            for half in range(2):
                for step in range(2):
                    cp = spread_copy(color, half, step, 0)
                    cp.start()
                    sends.append(cp)
        for color in range(3):
            for half in range(2):
                first, second = halves[half]
                spread_arrival(spread_copy, target, me, color, half, 0, first)
                cp = spread_copy(color, half, 2, first)
                cp.start()
                sends.append(cp)
        for color in range(3):
            for half in range(2):
                first, second = halves[half]
                spread_arrival(spread_copy, target, me, color, half, 1, second)
                spread_arrival(spread_copy, target, me, color, half, 2, first | second)
    for cp in sends:
        cp.wait_send()
    for cp in locals_:
        cp.wait()


def spread_arrival(spread_copy, target, me, color, half, step, bits):
    spread_copy(color, half, step, bits).wait_recv()


def reduce_all(arrays, views, out_shapes, piece_shapes, spread, collective_id):
    any_spec = pl.BlockSpec(memory_space=pl.ANY)
    scratch = []
    for count in (8, 8, 7):
        for shape in piece_shapes:
            scratch.append(pltpu.VMEM((count,) + shape, F32))
    sems = [pltpu.SemaphoreType.DMA((24,))] * 5 + [pltpu.SemaphoreType.DMA((3,))] + [pltpu.SemaphoreType.DMA((18,))] * 2
    return pl.pallas_call(
        functools.partial(reduce_kernel, views, spread),
        out_shape=[jax.ShapeDtypeStruct(s, F32) for s in out_shapes],
        in_specs=[any_spec] * len(arrays), out_specs=[any_spec] * 3,
        scratch_shapes=scratch + sems,
        compiler_params=pltpu.CompilerParams(collective_id=collective_id, has_side_effects=True, vmem_limit_bytes=VMEM_LIMIT),
        name=f"reduce_all_{collective_id}",
    )(*arrays)


def logits_kernel(chunks, vocab, hn_ref, emb_ref, lab_ref, z_ref, st_ref):
    hn = hn_ref[...]
    lab = lab_ref[...]
    top = None
    lab_z = None
    for lo, count in chunks:
        z = lax.dot_general(hn, emb_ref[lo:lo + count, :], (((1,), (1,)), ((), ())), preferred_element_type=F32)
        z_ref[:, lo:lo + count] = z
        col = lax.broadcasted_iota(jnp.int32, z.shape, 1) + lo
        picked = jnp.sum(jnp.where(col == lab, z, 0.0), axis=1, keepdims=True)
        if lo + count > vocab:
            z = jnp.where(col < vocab, z, -jnp.inf)
        peak = jnp.max(z, axis=1, keepdims=True)
        top = peak if top is None else jnp.maximum(top, peak)
        lab_z = picked if lab_z is None else lab_z + picked
    total = None
    for lo, count in chunks:
        z = z_ref[:, lo:lo + count]
        e = jnp.exp(z - top)
        if lo + count > vocab:
            col = lax.broadcasted_iota(jnp.int32, z.shape, 1) + lo
            e = jnp.where(col < vocab, e, 0.0)
        part = jnp.sum(e, axis=1, keepdims=True)
        total = part if total is None else total + part
    lane = lax.broadcasted_iota(jnp.int32, st_ref.shape, 1)
    st_ref[...] = jnp.where(lane == 0, top, jnp.where(lane == 1, total, lab_z))


def grads_kernel(chunks, vocab, inv_n, z_ref, hn_ref, emb_ref, st_ref, lab_ref, dhn_ref, de_ref):
    @pl.when(pl.program_id(0) == 0)
    def _():
        de_ref[...] = jnp.zeros_like(de_ref)

    hn = hn_ref[...]
    lab = lab_ref[...]
    top = st_ref[:, 0:1]
    inv_sum = 1.0 / st_ref[:, 1:2]
    acc = None
    for lo, count in chunks:
        z = z_ref[:, lo:lo + count]
        p = jnp.exp(z - top) * inv_sum
        col = lax.broadcasted_iota(jnp.int32, z.shape, 1) + lo
        p = jnp.where(col == lab, p - 1.0, p) * inv_n
        if lo + count > vocab:
            p = jnp.where(col < vocab, p, 0.0)
        dz = p.astype(BF)
        part = jnp.dot(dz, emb_ref[lo:lo + count, :], preferred_element_type=F32)
        acc = part if acc is None else acc + part
        de_ref[lo:lo + count, :] += lax.dot_general(dz, hn, (((0,), (0,)), ((), ())), preferred_element_type=F32)
    dhn_ref[...] = acc


def make_chunks(padded):
    tiles = padded // 256
    out, lo = [], 0
    while tiles:
        take = 4 if tiles % 3 else 3
        take = min(take, tiles)
        out.append((lo, take * 256))
        lo += take * 256
        tiles -= take
    return tuple(out)


def head_logits(hn, emb, labels, vocab, block):
    n, d = hn.shape
    padded = emb.shape[0]
    return pl.pallas_call(
        functools.partial(logits_kernel, make_chunks(padded), vocab),
        grid=(n // block,),
        in_specs=[pl.BlockSpec((block, d), lambda i: (i, 0)),
                  pl.BlockSpec((padded, d), lambda i: (0, 0), pipeline_mode=pl.Buffered(1)),
                  pl.BlockSpec((block, 1), lambda i: (i, 0))],
        out_specs=[pl.BlockSpec((block, padded), lambda i: (i, 0)), pl.BlockSpec((block, 128), lambda i: (i, 0))],
        out_shape=[jax.ShapeDtypeStruct((n, padded), F32), jax.ShapeDtypeStruct((n, 128), F32)],
        compiler_params=pltpu.CompilerParams(vmem_limit_bytes=VMEM_LIMIT),
        cost_estimate=pl.CostEstimate(flops=2 * n * d * padded, bytes_accessed=4 * n * padded, transcendentals=n * padded),
        name="head_logits",
    )(hn, emb, labels)


def head_grads(z, hn, emb, stats, labels, vocab, inv_n, block):
    n, d = hn.shape
    padded = emb.shape[0]
    return pl.pallas_call(
        functools.partial(grads_kernel, make_chunks(padded), vocab, inv_n),
        grid=(n // block,),
        in_specs=[pl.BlockSpec((block, padded), lambda i: (i, 0)),
                  pl.BlockSpec((block, d), lambda i: (i, 0)),
                  pl.BlockSpec((padded, d), lambda i: (0, 0), pipeline_mode=pl.Buffered(1)),
                  pl.BlockSpec((block, 2), lambda i: (i, 0)),
                  pl.BlockSpec((block, 1), lambda i: (i, 0))],
        out_specs=[pl.BlockSpec((block, d), lambda i: (i, 0)),
                   pl.BlockSpec((padded, d), lambda i: (0, 0), pipeline_mode=pl.Buffered(1))],
        out_shape=[jax.ShapeDtypeStruct((n, d), F32), jax.ShapeDtypeStruct((padded, d), F32)],
        compiler_params=pltpu.CompilerParams(vmem_limit_bytes=VMEM_LIMIT),
        cost_estimate=pl.CostEstimate(flops=4 * n * d * padded, bytes_accessed=4 * n * padded, transcendentals=n * padded),
        name="head_grads",
    )(z, hn, emb, stats, labels)


def mlp_forward(x_emb, gain_in, w_gate, w_up, w_down):
    normed_in, norm_in_back = jax.vjp(lambda values: rms_scale(values, gain_in), x_emb)
    normed_bf = normed_in.astype(BF)
    gate_f = jnp.dot(normed_bf, w_gate, preferred_element_type=F32).astype(BF).astype(F32)
    up_f = jnp.dot(normed_bf, w_up, preferred_element_type=F32).astype(BF).astype(F32)
    gate_sig = jax.nn.sigmoid(gate_f)
    silu_gate = gate_f * gate_sig
    act_bf = (silu_gate * up_f).astype(BF)
    mlp_out = jnp.dot(act_bf, w_down, preferred_element_type=F32).astype(BF)
    h_res = x_emb + mlp_out.astype(F32)
    return h_res, (norm_in_back, normed_bf, gate_f, up_f, gate_sig, silu_gate, act_bf)


def mlp_backward(d_hidden, saved, w_gate, w_up, w_down):
    norm_in_back, normed_bf, gate_f, up_f, gate_sig, silu_gate, act_bf = saved
    d_mlp = d_hidden.astype(BF)
    d_act = jnp.einsum("td,fd->tf", d_mlp, w_down, preferred_element_type=F32)
    grad_down = jnp.einsum("tf,td->fd", act_bf, d_mlp, preferred_element_type=F32)
    d_gate = (d_act * up_f * (gate_sig * (1.0 + gate_f * (1.0 - gate_sig)))).astype(BF)
    d_up = (d_act * silu_gate).astype(BF)
    grad_gate = jnp.einsum("td,tf->df", normed_bf, d_gate, preferred_element_type=F32)
    grad_up = jnp.einsum("td,tf->df", normed_bf, d_up, preferred_element_type=F32)
    d_normed = jnp.einsum("tf,df->td", d_gate, w_gate, preferred_element_type=F32) + jnp.einsum("tf,df->td", d_up, w_up, preferred_element_type=F32)
    d_x = d_hidden + norm_in_back(d_normed)[0]
    return d_x, grad_gate, grad_up, grad_down


HN_PARTS = ((0, 176), (176, 176), (352, 160))
STAT_PARTS = ((0, 8), (8, 8), (16, 8))


def solution(mesh):
    tok_spec = P("fsdp", None)
    row_spec = P(AXES, None)
    weight_spec = P("fsdp", None)

    def device_step(tok_ids, tok_labels, table_shard, gate_shard, up_shard, down_shard, gain_in, gain_out):
        m_idx = lax.axis_index("model")
        f_idx = lax.axis_index("fsdp")
        me = m_idx * 4 + f_idx
        vocab, width = table_shard.shape
        own = tok_ids.shape[0] * tok_ids.shape[1] // 4
        num_tokens = own * 16

        def full_weight(shard):
            rows = shard.shape[0] // 4
            piece = lax.dynamic_slice_in_dim(shard, m_idx * rows, rows, axis=0)
            return lax.all_gather(piece, ("fsdp", "model"), axis=0, tiled=True)

        w_gate, w_up, w_down = full_weight(gate_shard), full_weight(up_shard), full_weight(down_shard)
        tokens = lax.all_gather(jnp.stack([tok_ids.reshape(-1), tok_labels.reshape(-1)]), "fsdp", axis=0)
        tokens = tokens.reshape(4, 2, 4, own).transpose(1, 2, 0, 3).reshape(2, 16, own)
        ids, labels = tokens[0], tokens[1].reshape(num_tokens)
        my_ids = lax.dynamic_slice_in_dim(ids, me, 1, axis=0)[0]

        mine = (ids // vocab) == me
        place = lax.broadcasted_iota(jnp.int32, ids.shape, 1)
        picked = lax.sort(jnp.where(mine, place, place + own), dimension=1)
        owner = my_ids // vocab
        owner_hot = (owner[:, None] == jnp.arange(16, dtype=jnp.int32)[None, :])
        counts = jnp.cumsum(owner_hot.astype(jnp.int32), axis=0)
        rank = jnp.sum(jnp.where(owner_hot, counts, 0), axis=1) - 1
        hot_all = (ids // vocab)[:, :, None] == jnp.arange(16, dtype=jnp.int32)
        most = jnp.max(jnp.sum(hot_all.astype(jnp.int32), axis=1))
        rounds = (most + ROUND_ROWS - 1) // ROUND_ROWS

        def served(r):
            pos = lax.dynamic_slice(jnp.pad(picked, ((0, 0), (0, ROUND_ROWS)), constant_values=2 * own), (0, r * ROUND_ROWS), (16, ROUND_ROWS))
            valid = pos < own
            safe = jnp.where(valid, pos, 0)
            row = jnp.take_along_axis(ids, safe, axis=1) - me * vocab
            return valid, jnp.where(valid, row, 0)

        def lookup_round(state):
            r, x = state
            _, row = served(r)
            sent = jnp.take(table_shard, row.reshape(-1), axis=0)
            got = lax.all_to_all(sent, AXES, split_axis=0, concat_axis=0, tiled=True)
            at = rank - r * ROUND_ROWS
            now = (at >= 0) & (at < ROUND_ROWS)
            fetched = jnp.take(got, jnp.where(now, owner * ROUND_ROWS + at, 0), axis=0)
            return r + 1, jnp.where(now[:, None], fetched, x)

        _, x_rows = lax.while_loop(lambda s: s[0] < rounds, lookup_round, (jnp.int32(0), jnp.zeros((own, width), BF)))
        x_emb = x_rows.astype(F32)

        h_res, saved = mlp_forward(x_emb, gain_in, w_gate, w_up, w_down)
        hn_f, norm_out_back = jax.vjp(lambda values: rms_scale(values, gain_out), h_res)
        hn_bf = gather_all(hn_f.astype(BF), HN_PARTS, 0)

        padded = (vocab + 255) // 256 * 256
        emb = jnp.pad(table_shard, ((0, padded - vocab), (0, 0)))
        loc_labels = (labels - me * vocab)
        in_here = (loc_labels >= 0) & (loc_labels < vocab)
        lab_col = jnp.where(in_here, loc_labels, -1).reshape(num_tokens, 1)
        z, local_stats = head_logits(hn_bf, emb, lab_col, vocab, 512)
        packed = local_stats[:, :3].T.reshape(24, num_tokens // 8)
        all_stats = gather_all(packed, STAT_PARTS, 1).reshape(16, 3, num_tokens)
        tops = all_stats[:, 0]
        row_max = jnp.max(tops, axis=0)
        sum_exp = jnp.sum(all_stats[:, 1] * jnp.exp(tops - row_max[None, :]), axis=0)
        label_logit = jnp.sum(all_stats[:, 2], axis=0)
        loss = jnp.sum(row_max + jnp.log(sum_exp) - label_logit) / num_tokens
        stat_cols = jnp.stack([row_max, sum_exp], axis=1)
        dhn_part, d_head = head_grads(z, hn_bf, emb, stat_cols, lab_col, vocab, 1.0 / num_tokens, 256)

        hn_views = tuple((0, count, lambda m, f, lo=lo: (m * 4 + f) * own + lo) for lo, count in HN_PARTS)
        shapes = [(count, width) for _, count in HN_PARTS]
        d_hn = jnp.concatenate(reduce_all([dhn_part], hn_views, shapes, shapes, None, 2), axis=0)
        d_hidden = norm_out_back(d_hn)[0]
        d_x, g_gate, g_up, g_down = mlp_backward(d_hidden, saved, w_gate, w_up, w_down)

        def grad_round(state):
            r, grad = state
            at = rank - r * ROUND_ROWS
            now = (at >= 0) & (at < ROUND_ROWS)
            slot = jnp.where(now, owner * ROUND_ROWS + at, 16 * ROUND_ROWS)
            source = jnp.zeros((16 * ROUND_ROWS + 1,), jnp.int32).at[slot].set(jnp.arange(own, dtype=jnp.int32))[:-1]
            sent = jnp.take(d_x, source, axis=0)
            got = lax.all_to_all(sent, AXES, split_axis=0, concat_axis=0, tiled=True)
            valid, row = served(r)
            valid, row = valid.reshape(-1), row.reshape(-1)
            return r + 1, grad.at[row].add(jnp.where(valid[:, None], got, 0.0))

        _, grad_table = lax.while_loop(lambda s: s[0] < rounds, grad_round, (jnp.int32(0), d_head[:vocab]))

        g_rows, d_rows = w_gate.shape[0] // 16, w_down.shape[0] // 16
        views = (
            (0, g_rows, lambda m, f: f * (4 * g_rows) + m * g_rows),
            (1, g_rows, lambda m, f: f * (4 * g_rows) + m * g_rows),
            (2, d_rows, lambda m, f: f * (4 * d_rows) + m * d_rows),
        )
        pieces = [(g_rows, w_gate.shape[1]), (g_rows, w_gate.shape[1]), (d_rows, w_down.shape[1])]
        grad_gate, grad_up, grad_down = reduce_all(
            [g_gate, g_up, g_down], views, [(4 * r, c) for r, c in pieces], pieces, True, 3)
        return loss, grad_table, grad_gate, grad_up, grad_down

    return jax.shard_map(device_step, mesh=mesh, in_specs=(tok_spec, tok_spec, row_spec, weight_spec, weight_spec, weight_spec, P(), P()), out_specs=(P(), row_spec, weight_spec, weight_spec, weight_spec), check_vma=False)
```

time: 1260 us -> 819 us (0.65)
  waiting for transfers between devices: 713 us -> 98.6 us
  Pallas kernels: 0 us -> 501 us
  matrix products: 327 us -> 51.8 us
  other arithmetic: 139 us -> 43.8 us
  local copies, waits for them, and re-layouts: 31.4 us -> 82.8 us
  blocking collectives: 31.3 us -> 6.45 us
    pallas_call x0 -> x6, Pallas kernels: none -> 501 us  [the longest x2 249 us: reduce_all(): pl.pallas_call(functools.partial(reduce_kernel, views, spread), out_shape...]
    dot_general x12 -> x9, matrix products: 327 us -> 51.8 us  [the longest x1 9.48 us: mlp_backward(): jnp.einsum('tf,td->fd', act_bf, d_mlp, preferred_element_type=F32)]
    unnamed x11 -> x3, waiting for transfers between devices: 264 us -> 0.05 us
    psum x2 -> x0, waiting for transfers between devices: 205 us -> none  [the longest x1 129 us: device_step(): lax.psum(jnp.einsum('tv,vd->td', d_logits, table_part, preferred_element_...]
    all_gather x4 -> x3, waiting for transfers between devices: 194 us -> 43.6 us  [full_weight(): return lax.all_gather(piece, ('fsdp', 'model'), axis=0, tiled=True)]
    all_to_all x0 -> x2, waiting for transfers between devices: none -> 54.9 us  [the longest x1 30.8 us: grad_round(): got = lax.all_to_all(sent, AXES, split_axis=0, concat_axis=0, tiled=True)]
    reduce_scatter x3 -> x0, waiting for transfers between devices: 50.3 us -> none  [the longest x1 50.2 us: device_step(): lax.psum_scatter(grad_down, 'fsdp', scatter_dimension=0, tiled=True)]
    convert_element_type x1 -> x2, other arithmetic: 50.2 us -> 1.08 us  [the longest x1 1.08 us: device_step(): hn_bf = gather_all(hn_f.astype(BF), HN_PARTS, 0)]
  transfers between devices with their start and end apart: 10 -> 5, of which waited for: 8 -> 4; matrix products, arithmetic and copies ran while one was open for 17% -> 8% of each run, Pallas kernels for 0% -> 0%
where the time goes in v1:
time: 819 us; the launch traced here: 813 us
  Pallas kernels  501 us (61%)
  waiting for transfers between devices  98.6 us (12%)
  local copies, waits for them, and re-layouts  82.8 us (10%)
  matrix products  51.8 us (6%)
  other arithmetic  43.8 us (5%)
  between operations  19.2 us (2%)
    pallas_call x2, Pallas kernels, reduce_all(): pl.pallas_call(functools.partial(reduce_kernel, views, spread), out_shape...  249 us
    pallas_call x1, Pallas kernels, head_grads(): pl.pallas_call(functools.partial(grads_kernel, make_chunks(padded), vocab...  125 us
    pallas_call x1, Pallas kernels, head_logits(): pl.pallas_call(functools.partial(logits_kernel, make_chunks(padded), voca...  68.3 us
    pallas_call x2, Pallas kernels, gather_all(): pl.pallas_call(functools.partial(gather_kernel, parts, rows), out_shape=j...  58.9 us
    all_gather x3, waiting for transfers between devices, full_weight(): return lax.all_gather(piece, ('fsdp', 'model'), axis=0, tiled=True)  43.6 us
    all_to_all x1, waiting for transfers between devices, grad_round(): got = lax.all_to_all(sent, AXES, split_axis=0, concat_axis=0, tiled=True)  30.8 us
    all_to_all x1, waiting for transfers between devices, lookup_round(): got = lax.all_to_all(sent, AXES, split_axis=0, concat_axis=0, tiled=True)  24.1 us
    gather x6, local copies, waits for them, and re-layouts, served(): row = jnp.take_along_axis(ids, safe, axis=1) - me * vocab  17.4 us
  transfers between devices with their start and end apart: 5, of which 4 were waited for; matrix products, arithmetic and copies ran while one was open for 8% of the time, Pallas kernels for 0%

profile of v1, /device:TPU:0, one launch (start us, length us, event | category | flops | bytes accessed | tf_op | source)
XLA Modules:
  0.0 812.6 jit_solution(5523314788096182783)
XLA Ops:
  8.1 0.7 add_bitcast_fusion.1
  8.8 6.4 all-gather.1
  15.4 0.6 iota_select_fusion
  16.1 1.7 constant_dynamic-slice_fusion.1
  17.9 1.7 constant_dynamic-slice_fusion.2
  19.7 1.7 constant_dynamic-slice_fusion
  21.5 0.4 convert_reduce_fusion
  21.9 0.6 reduce_max.18
  23.2 1.2 reduce-window.6
  24.7 5.3 sub.131
  30.0 4.7 and_select_fusion.lab_ref
  34.7 5.0 pad.15.emb_ref
  39.8 49.6 %while.24 = (s32[]{:T(128)}, bf16[512,768]{1,0:T(8,128)(2,1)S(1)}, s32[]{:T(128)}, s32[512]{0:T(512)S(1)}, s32[512]{0:T(512)S(1)}, /*index=5*/s32[16,512]{1,0:T(...) while((s32[]{:T(128)}, bf16[512,768]{1,0:T(8,128)(2,1)S(1)}, ...), condition=%wide.region_7.9_spmd, body=%wide.region_6.8_spmd.sunk | while | flops 1613830 | bytes 15235319 | solution.py:505
  39.8 0.8 bitcast_or_fusion.4
  40.7 8.6 %gather_fusion = s32[1024]{0:T(1024)S(1)} fusion(s32[16,512]{1,0:T(8,128)S(1)} %get-tuple-element.459, s32[1024]{0:T(1024)S(1)} %reshape.509), kind=kCustom, calls=%fused_computation.clone.clone.1 | custom fusion | bytes 16384 | tf_op jit(solution)/shard_map/while/body/jit(take_along_axis)/gather | solution.py:492
  49.5 7.5 gather_fusion.1
  57.0 1.4 broadcast_select_fusion.4
  58.4 4.1 all-to-all-start
  62.5 24.1 %all-to-all-done = bf16[16,64,768]{2,1,0:T(8,128)(2,1)S(1)} async-done(((bf16[16,64,768]{2,1,0:T(8,128)(2,1)}), bf16[16,64,768]{2,1,0:T(8,128)(2,1)S(1)}, u32[]{:S(2)}, u32[]{:S(2)}) %all-to-all-start) | async-done | bytes 1572896 | tf_op jit(solution)/shard_map/while/body/all_to_all | solution.py:499
  86.6 2.0 gather_fusion.2
  89.8 6.5 convolution_convert_fusion
  96.3 10.8 %all-gather.6.cloned.1.call-done = bf16[768,3072]{1,0:T(8,128)(2,1)} async-done(((bf16[48,3072]{1,0:T(8,128)(2,1)}), bf16[768,3072]{1,0:T(8,128)(2,1)}) %all-gather.6.cloned.1.call-update) | async-done | bytes 4718608 | tf_op jit(solution)/shard_map/all_gather | solution.py:469
  107.1 6.5 convolution_convert_fusion.1
  113.6 32.8 %all-gather.10.cloned.1.call-done = bf16[3072,768]{1,0:T(8,128)(2,1)} async-done(((bf16[192,768]{1,0:T(8,128)(2,1)}), bf16[3072,768]{1,0:T(8,128)(2,1)}) %all-gather.10.cloned.1.call-update) | async-done | bytes 4718608 | tf_op jit(solution)/shard_map/all_gather | solution.py:469
  146.4 7.4 multiply_reduce_fusion.1
  153.8 1.1 copy-done.6
  154.9 1.1 multiply_convert_fusion.1.in_ref
  156.0 46.4 %gather_all_0.1.hn_ref = bf16[8192,768]{1,0:T(8,128)(2,1)} custom-call(bf16[512,768]{1,0:T(8,128)(2,1)} %multiply_convert_fusion.1.in_ref), custom_call_target="tpu_custom_call" | custom-call | tf_op jit(solution)/shard_map/gather_all_0/pallas_call | solution.py:145
  202.4 68.3 %head_logits.1 = (f32[8192,3328]{1,0:T(8,128)}, f32[8192,128]{1,0:T(8,128)}) custom-call(bf16[8192,768]{1,0:T(8,128)(2,1)} %gather_all_0.1.hn_ref, bf16[3328,768]{1,0:T(8,128)(2,1)} %pad.15.emb_ref, s32[8192,1]{1,0:T(8,128)} %and_select_fusion.lab_ref), custom_call_target="tpu_custom_call" | custom-call | flops 41875931136 | bytes 109051904 | tf_op jit(solution)/shard_map/head_logits/pallas_call | solution.py:388
  270.8 4.4 slice_bitcast_fusion
  275.1 2.8 copy.38
  278.0 0.7 reshape.397.in_ref
  278.7 12.5 %gather_all_1.1 = f32[384,1024]{1,0:T(8,128)} custom-call(f32[24,1024]{1,0:T(8,128)} %reshape.397.in_ref), custom_call_target="tpu_custom_call" | custom-call | tf_op jit(solution)/shard_map/gather_all_1/pallas_call | solution.py:145
  291.2 3.0 reshape.398
  294.2 1.4 slice_reduce_fusion.2
  295.6 0.7 fusion.20
  296.3 0.6 subtract_reduce_fusion
  297.0 2.6 copy.40.st_ref
  299.6 124.9 %head_grads.1 = (f32[8192,768]{1,0:T(8,128)}, f32[3328,768]{1,0:T(8,128)}) custom-call(f32[8192,3328]{1,0:T(8,128)} %get-tuple-element.234.z_ref, bf16[8192,768]{1,0:T(8,128)(2,1)} %gather_all_0.1.hn_ref, bf16[3328,768]{1,0:T(8,128)(2,1)} %pad.15.emb_ref, f32[8192,2]{1,0:T(8,128)} %copy.40.st_ref, s32[8192,1]{1,0:T(8,128)} %and_select_fusion.lab_ref), custom_call_target="tpu_custom_call" | custom-call | flops 83751862272 | bytes 109051904 | tf_op jit(solution)/shard_map/head_grads/pallas_call | solution.py:405
  424.4 8.2 %slice.44 = f32[3144,768]{1,0:T(8,128)} slice(f32[3328,768]{1,0:T(8,128)} %get-tuple-element.235), slice={[0:3144], [0:768]} | slice | bytes 19316736 | tf_op jit(solution)/shard_map/slice | solution.py:546
  432.6 92.2 %reduce_all_2.1 = (f32[176,768]{1,0:T(8,128)}, f32[176,768]{1,0:T(8,128)}, f32[160,768]{1,0:T(8,128)}) custom-call(f32[8192,768]{1,0:T(8,128)} %get-tuple-element.236.refs_0_), custom_call_target="tpu_custom_call" | custom-call | tf_op jit(solution)/shard_map/reduce_all_2/pallas_call | solution.py:311
  524.9 2.2 multiply_reduce_fusion
  527.9 1.2 copy-done.30
  529.1 9.5 %fusion.21.refs_2_ = f32[3072,768]{1,0:T(8,128)} fusion(f32[512,768]{1,0:T(8,128)S(1)} %add_add_fusion.1, bf16[512,3072]{1,0:T(8,128)(2,1)S(1)} %copy-done.30, bf16[512,3072]{1,0:T(8,128)(2,1)} %convolution_convert_fusion.1), kind=kOutput, calls=%fused_computation.86 | convolution fusion | flops 2428895232 | bytes 17301504 | tf_op jit(solution)/shard_map/tf,td->fd/dot_general | solution.py:439
  538.7 4.7 multiply_convert_fusion
  543.4 5.3 fusion.33.refs_0_
  548.7 5.5 fusion.31.refs_1_
  554.2 2.7 fusion.40
  557.0 3.8 fusion.16
  560.8 157.1 %reduce_all_3.1 = (f32[192,3072]{1,0:T(8,128)}, f32[192,3072]{1,0:T(8,128)}, f32[768,768]{1,0:T(8,128)}) custom-call(f32[768,3072]{1,0:T(8,128)} %fusion.33.refs_0_, f32[768,3072]{1,0:T(8,128)} %fusion.31.refs_1_, f32[3072,768]{1,0:T(8,128)} %fusion.21.refs_2_), custom_call_target="tpu_custom_call" | custom-call | tf_op jit(solution)/shard_map/reduce_all_3/pallas_call | solution.py:311
  718.6 2.5 fusion.12
  721.2 74.9 %while.25 = (s32[]{:T(128)}, f32[3144,768]{1,0:T(8,128)}, s32[]{:T(128)}, s32[16,512]{1,0:T(8,128)S(1)}, s32[16,512]{1,0:T(8,128)S(1)}, /*index=5*/s32[]{:T(128)...) while((s32[]{:T(128)}, f32[3144,768]{1,0:T(8,128)}, ...), condition=%wide.region_19.21_spmd, body=%wide.region_16.20_spmd.sunk | while | flops 2400262 | bytes 37964008 | solution.py:546
  721.2 2.5 scatter_custom_fusion.7
  723.8 5.3 gather_fusion.4
  729.0 3.9 broadcast_select_fusion.5
  732.9 3.6 all-to-all-start.1
  736.9 8.6 %gather_fusion.3 = s32[1024]{0:T(1024)S(1)} fusion(s32[16,512]{1,0:T(8,128)S(1)} %get-tuple-element.496, s32[1024]{0:T(1024)S(1)} %reshape.520), kind=kCustom, calls=%fused_computation.3.clone.clone.1 | custom fusion | bytes 16384 | tf_op jit(solution)/shard_map/while/body/jit(take_along_axis)/gather | solution.py:492
  745.7 30.8 %all-to-all-done.1 = f32[16,64,768]{2,1,0:T(8,128)} async-done(((f32[16,64,768]{2,1,0:T(8,128)}), f32[16,64,768]{2,1,0:T(8,128)}, u32[]{:S(2)}, u32[]{:S(2)}) %all-to-all-start.1) | async-done | bytes 3145760 | tf_op jit(solution)/shard_map/while/body/all_to_all | solution.py:541
  776.5 3.8 bitcast_select_fusion.2
  780.4 15.7 %scatter_fusion = f32[3144,768]{1,0:T(8,128)} fusion(f32[3144,768]{1,0:T(8,128)} %get-tuple-element.480, s32[1024]{0:T(1024)S(1)} %bitcast.99, f32[1024,768]{1,0:T(8,128)} %bitcast_select_fusion.2), kind=kCustom, calls=%fused_computation.6.clone.1 | custom fusion | flops 786432 | bytes 9441280 | tf_op jit(solution)/shard_map/while/body/scatter-add | solution.py:544
  796.0 3.4 copy.74
  799.5 1.4 copy.75
  800.9 1.1 copy-done.9
  802.0 1.4 copy.76
  (133 shorter events, 3.5 us)
Async XLA Ops:
  8.0 31.7 %sort.9.cloned.1.call-start = ((), (), s32[]{:S(2)}) async-start(), calls=%async_computation.5 | async-start | bytes 98336 | tf_op jit(solution)/shard_map/sort | solution.py:479
  16.1 73.7 %all-gather.8.cloned.1.call-start = ((), (), s32[]{:S(2)}) async-start(), calls=%async_computation.3 | async-start | bytes 5013504 | tf_op jit(solution)/shard_map/all_gather | solution.py:469
  17.9 89.2 %all-gather.6.cloned.1.call-start = ((), (), s32[]{:S(2)}) async-start(), calls=%async_computation.2 | async-start | bytes 5013504 | tf_op jit(solution)/shard_map/all_gather | solution.py:469
  19.6 126.7 %all-gather.10.cloned.1.call-start = ((), (), s32[]{:S(2)}) async-start(), calls=%async_computation.4 | async-start | bytes 5013504 | tf_op jit(solution)/shard_map/all_gather | solution.py:469
  39.8 50.0 %copy-start.14 = (f32[768]{0:T(1024)S(1)}, f32[768]{0:T(1024)}, u32[]{:S(2)}) copy-start(f32[768]{0:T(1024)} %param.20) | copy-start | bytes 9220
  40.7 8.7 %copy-start.4 = (s32[16,512]{1,0:T(8,128)S(1)}, s32[16,512]{1,0:T(8,128)}, u32[]{:S(2)}) copy-start(s32[16,512]{1,0:T(8,128)} %get-tuple-element.458) | copy-start | bytes 98308 | tf_op jit(solution)/shard_map/while
  58.4 28.2 %all-to-all-start = ((bf16[16,64,768]{2,1,0:T(8,128)(2,1)}), bf16[16,64,768]{2,1,0:T(8,128)(2,1)S(1)}, u32[]{:S(2)}, u32[]{:S(2)}) async-start(bf16[16,64,768]{2,1,0:T(8,128)(2,1)} %broadcast_select_fusion.4), calls=%async_computation | async-start | bytes 3145728 | tf_op jit(solution)/shard_map/while/body/all_to_all | solution.py:499
  89.4 6.8 copy-start
  89.4 6.8 copy-start.18
  89.4 6.8 copy-start.20
  89.5 56.9 %copy-start.2 = (bf16[512,768]{1,0:T(8,128)(2,1)}, bf16[512,768]{1,0:T(8,128)(2,1)S(1)}, u32[]{:S(2)}) copy-start(bf16[512,768]{1,0:T(8,128)(2,1)S(1)} %get-tuple-element.232) | copy-start | bytes 2359300
  89.7 6.6 copy-start.24
  89.7 17.3 %copy-start.16 = (f32[512]{0:T(512)}, f32[512]{0:T(512)S(1)}, u32[]{:S(2)}) copy-start(f32[512]{0:T(512)S(1)} %fusion.29) | copy-start | bytes 6148
  113.6 41.3 %copy-start.22 = (f32[768]{0:T(1024)S(1)}, f32[768]{0:T(1024)}, u32[]{:S(2)}) copy-start(f32[768]{0:T(1024)} %param.21) | copy-start | bytes 9220
  153.8 1.1 copy-start.6
  153.8 48.7 %copy-start.28 = (f32[512]{0:T(512)}, f32[512]{0:T(512)S(1)}, u32[]{:S(2)}) copy-start(f32[512]{0:T(512)S(1)} %get-tuple-element.297) | copy-start | bytes 6148
  153.8 48.6 %copy-start.26 = (f32[512]{0:T(512)}, f32[512]{0:T(512)S(1)}, u32[]{:S(2)}) copy-start(f32[512]{0:T(512)S(1)} %fusion.30) | copy-start | bytes 6148
  432.6 92.3 %copy-start.23 = (f32[768]{0:T(1024)S(1)}, f32[768]{0:T(1024)}, u32[]{:S(2)}) copy-start(f32[768]{0:T(1024)} %param.21) | copy-start | bytes 9220
  524.8 2.3 copy-start.29
  524.8 2.4 copy-start.7
  524.8 2.5 copy-start.11
  524.8 2.6 copy-start.12
  524.8 2.7 copy-start.13
  524.9 2.7 copy-start.27
  527.1 2.0 copy-start.30
  527.6 11.0 %slice-start.4 = ((s8[4718592]{0:T(1024)(128)(4,1)}), s8[4194304]{0:T(1024)(128)(4,1)S(1)}, s32[]{:S(2)}) async-start(s8[4718592]{0:T(1024)(128)(4,1)} %bitcast.112), calls=%async_computation.11 | async-start | bytes 8388608
  529.1 9.5 %copy-start.8 = (f32[512,768]{1,0:T(8,128)}, f32[512,768]{1,0:T(8,128)S(1)}, u32[]{:S(2)}) copy-start(f32[512,768]{1,0:T(8,128)S(1)} %add_add_fusion.1) | copy-start | bytes 4718596
  529.1 9.5 %slice-start.5 = ((s8[4718592]{0:T(1024)(128)(4,1)}), s8[524288]{0:T(1024)(128)(4,1)S(1)}, s32[]{:S(2)}) async-start(s8[4718592]{0:T(1024)(128)(4,1)} %bitcast.112), calls=%async_computation.12 | async-start | bytes 1048576
  529.1 9.5 %copy-start.31 = (bf16[512,3072]{1,0:T(8,128)(2,1)S(1)}, bf16[512,3072]{1,0:T(8,128)(2,1)}, u32[]{:S(2)}) copy-start(bf16[512,3072]{1,0:T(8,128)(2,1)} %convolution_convert_fusion.1) | copy-start | bytes 9437188
  538.6 4.8 copy-start.3
  538.7 4.7 copy-start.15
  538.7 4.7 copy-start.17
  543.4 10.8 %slice-start.2 = ((s8[4718592]{0:T(1024)(128)(4,1)}), s8[4194304]{0:T(1024)(128)(4,1)S(1)}, s32[]{:S(2)}) async-start(s8[4718592]{0:T(1024)(128)(4,1)} %bitcast.110), calls=%async_computation.9 | async-start | bytes 8388608
  548.7 5.5 slice-start.3
  548.7 8.2 %slice-start = ((s8[4718592]{0:T(1024)(128)(4,1)}), s8[4194304]{0:T(1024)(128)(4,1)S(1)}, s32[]{:S(2)}) async-start(s8[4718592]{0:T(1024)(128)(4,1)} %bitcast.108), calls=%async_computation.7 | async-start | bytes 8388608
  554.2 2.7 slice-start.1
  556.9 3.9 copy-start.25
  717.9 3.2 copy-start.1
  717.9 3.2 copy-start.5
  717.9 3.2 copy-start.19
  717.9 3.2 copy-start.21
  732.9 43.6 %all-to-all-start.1 = ((f32[16,64,768]{2,1,0:T(8,128)}), f32[16,64,768]{2,1,0:T(8,128)}, u32[]{:S(2)}, u32[]{:S(2)}) async-start(f32[16,64,768]{2,1,0:T(8,128)} %broadcast_select_fusion.5), calls=%async_computation.1 | async-start | bytes 6291456 | tf_op jit(solution)/shard_map/while/body/all_to_all | solution.py:541
  796.0 3.5 copy-start.10
  799.5 2.5 copy-start.9
Sparse Core Ops, SparseCore 0:
  16.2 2.7 sort.11.cloned.1.call-done
  (1 shorter events, 0.0 us)
Sparse Core Ops, SparseCore 1:
  18.8 38.3 all-gather.7
  59.2 47.8 all-gather.5
  109.8 36.6 all-gather.9

commit v2 on v0

v2 whole, which is shorter than its diff:
```python
import functools

import jax
import jax.numpy as jnp
from jax import lax
from jax.experimental import pallas as pl
from jax.experimental.pallas import tpu as pltpu
from jax.sharding import PartitionSpec as P

EPS = 1e-6
NT = (((1,), (1,)), ((), ()))
TN = (((0,), (0,)), ((), ()))
MESH = pl.DeviceIdType.MESH
AXES = ("model", "fsdp")
BF = jnp.bfloat16
F32 = jnp.float32
ROUND_ROWS = 56
VMEM_LIMIT = 66977792
ANY = pl.BlockSpec(memory_space=pl.ANY)
DMA = pltpu.SemaphoreType.DMA
DIMS = (1, 2, 4)
CHUNK = 8


def rms_scale(values, gain_vec):
    mean_sq = jnp.mean(values * values, axis=-1, keepdims=True)
    return values * lax.rsqrt(mean_sq + EPS) * gain_vec


def my_place():
    m = lax.axis_index("model")
    f = lax.axis_index("fsdp")
    return (f // 2, m % 2, m // 2, f % 2)


def flipped(place, bits, core=False):
    x, y, z, c = place
    if bits & 1:
        x = 1 - x
    if bits & 2:
        y = 1 - y
    if bits & 4:
        z = 1 - z
    if core:
        c = 1 - c
    return (x, y, z, c)


def mesh_id(place):
    x, y, z, c = place
    return (2 * z + y, 2 * x + c)


def greet(place, bit_list, core):
    barrier = pltpu.get_barrier_semaphore()
    peers = [flipped(place, b) for b in bit_list] + ([flipped(place, 0, True)] if core else [])
    for peer in peers:
        pl.semaphore_signal(barrier, inc=1, device_id=mesh_id(peer), device_id_type=MESH)
    pl.semaphore_wait(barrier, len(peers))


ORDERS = (DIMS, DIMS[1:] + DIMS[:1], DIMS[2:] + DIMS[:2])


def subsets(bits):
    out = [0]
    for b in bits:
        out = out + [o | b for o in out]
    return out


def device_of(place):
    m, f = mesh_id(place)
    return m * 4 + f


class Gather:
    def __init__(self, me, parts, rows, in_ref, out_ref, local_sem, send_sem, recv_sem, core_send, core_recv):
        self.me, self.parts, self.rows, self.in_ref, self.out_ref = me, parts, rows, in_ref, out_ref
        self.local_sem, self.sems, self.core_sems = local_sem, (send_sem, recv_sem), (core_send, core_recv)

    def part(self, place, color):
        lo, count = self.parts[color]
        return self.out_ref.at[pl.ds(pl.multiple_of(device_of(place) * self.rows + lo, CHUNK), count)]

    def copy(self, color, bits, core_src, peer, sems, k):
        lo, count = self.parts[color]
        dst = self.part(flipped(self.me, bits, core_src), color)
        src = dst if bits or core_src else self.in_ref.at[pl.ds(lo, count)]
        send, recv = sems
        return pltpu.make_async_remote_copy(
            src_ref=src, dst_ref=dst, send_sem=send.at[k], recv_sem=recv.at[k],
            device_id=mesh_id(peer), device_id_type=MESH)

    def chip(self, color, stage, held, arrival=False):
        order = ORDERS[color]
        k = color * CHUNK + (1 << stage) + subsets(order[:stage]).index(held)
        bits = held | order[stage] if arrival else held
        return self.copy(color, bits, False, flipped(self.me, order[stage]), self.sems, k)

    def core(self, color, bits, arrival=False):
        return self.copy(color, bits, arrival, flipped(self.me, 0, True), self.core_sems, color * CHUNK + bits)

    def local(self):
        at = pl.ds(pl.multiple_of(device_of(self.me) * self.rows, CHUNK), self.rows)
        return pltpu.make_async_copy(self.in_ref, self.out_ref.at[at], self.local_sem)

    def begin(self):
        greet(self.me, DIMS, True)
        self.local().start()
        for stage in range(3):
            for color in range(3):
                self.chip(color, stage, 0).start()
        for color in range(3):
            self.core(color, 0).start()

    def arrive(self, stage, index):
        for color in range(3):
            order = ORDERS[color]
            held = subsets(order[:stage])[index]
            self.chip(color, stage, held, True).wait_recv()
            bits = held | order[stage]
            for later in range(stage + 1, 3):
                self.chip(color, later, bits).start()
            self.core(color, bits).start()

    def core_arrive(self, bits):
        for color in range(3):
            self.core(color, bits, True).wait_recv()

    def finish(self):
        for color in range(3):
            for stage in range(3):
                for held in subsets(ORDERS[color][:stage]):
                    self.chip(color, stage, held).wait_send()
            for bits in range(8):
                self.core(color, bits).wait_send()
        self.local().wait()


def gather_sems():
    return [DMA] + [DMA((3 * CHUNK,))] * 4


def gather_kernel(parts, rows, *refs):
    g = Gather(my_place(), parts, rows, *refs)
    g.begin()
    for stage in range(3):
        for index in range(1 << stage):
            g.arrive(stage, index)
    for bits in range(8):
        g.core_arrive(bits)
    g.finish()


def gather_all(values, parts, collective_id):
    rows, width = values.shape
    return pl.pallas_call(
        functools.partial(gather_kernel, parts, rows),
        out_shape=jax.ShapeDtypeStruct((16 * rows, width), values.dtype),
        in_specs=[ANY], out_specs=ANY, scratch_shapes=gather_sems(),
        compiler_params=pltpu.CompilerParams(collective_id=collective_id, has_side_effects=True),
        name="gather_stats",
    )(values)


BLOCK_ORDER = (7, 6, 5, 3, 4, 2, 1, 0)


def add_rows(dst, slot_a, src, slot_b, lo, rows, chunk):
    def body(i, carry):
        at = pl.ds(pl.multiple_of(lo + i * chunk, 8), chunk)
        dst[slot_a, at, :] = dst[slot_a, at, :] + src[slot_b, at, :]
        return carry

    lax.fori_loop(0, rows // chunk, body, 0)


def stage_of(color, bits):
    order = ORDERS[color]
    for s in range(3):
        if bits & order[s]:
            return s
    return 3


def box_slot(color, stage, bits):
    rest = subsets(ORDERS[color][stage + 1:])
    return (0, 4, 6)[stage] + rest.index(bits)


def back_kernel(chunks, vocab, inv_n, parts, half, z_ref, emb_ref, st_ref, lab_ref, dz_ref, out_ref,
                acc, pairs, boxes, core_send, core_recv, send_sem, recv_sem, out_sem):
    i = pl.program_id(0)
    me = my_place()

    @pl.when(i == 0)
    def _():
        greet(me, DIMS, True)

    def core_copy(t):
        return pltpu.make_async_remote_copy(
            src_ref=acc.at[8 + t % 2], dst_ref=pairs.at[7 - t], send_sem=core_send.at[t], recv_sem=core_recv.at[t],
            device_id=mesh_id(flipped(me, 0, True)), device_id_type=MESH)

    def chip_copy(color, stage, bits):
        lo, count = parts[color]
        slot = box_slot(color, stage, bits & ~ORDERS[color][stage])
        k = color * 8 + slot
        return pltpu.make_async_remote_copy(
            src_ref=acc.at[bits, pl.ds(lo, count)], dst_ref=boxes.at[slot, pl.ds(lo, count)],
            send_sem=send_sem.at[k], recv_sem=recv_sem.at[k],
            device_id=mesh_id(flipped(me, ORDERS[color][stage])), device_id_type=MESH)

    for t in range(2, 8):
        @pl.when(i == 4 * t)
        def _(t=t):
            core_copy(t - 2).wait_send()

    lab = lab_ref[...]
    top = st_ref[:, 0:1]
    inv_sum = 1.0 / st_ref[:, 1:2]
    total = None
    for lo, count in chunks:
        z = z_ref[:, lo:lo + count]
        p = jnp.exp(z - top) * inv_sum
        col = lax.broadcasted_iota(jnp.int32, z.shape, 1) + lo
        p = jnp.where(col == lab, p - 1.0, p) * inv_n
        if lo + count > vocab:
            p = jnp.where(col < vocab, p, 0.0)
        dz = p.astype(BF)
        dz_ref[:, lo:lo + count] = dz
        part = jnp.dot(dz, emb_ref[lo:lo + count, :], preferred_element_type=F32)
        total = part if total is None else total + part
    t_now = i // 4
    own = (i // 2) % 2
    slot_now = own * (7 - t_now) + (1 - own) * (8 + t_now % 2)
    acc[slot_now, pl.ds(pl.multiple_of((i % 2) * half, half), half), :] = total

    for t in range(8):
        bits = 7 - t

        @pl.when(i == 4 * t + 1)
        def _(t=t):
            core_copy(t).start()

        @pl.when(i == 4 * t + 3)
        def _(t=t, bits=bits):
            core_copy(t).wait_recv()
            for color in range(3):
                lo, count = parts[color]
                add_rows(acc, bits, pairs, bits, lo, count, 16)
                mine = stage_of(color, bits)
                for s in range(mine):
                    chip_copy(color, s, bits | ORDERS[color][s]).wait_recv()
                    add_rows(acc, bits, boxes, box_slot(color, s, bits), lo, count, 16)
                if mine < 3:
                    chip_copy(color, mine, bits).start()

    @pl.when(i == 31)
    def _():
        done = pltpu.make_async_copy(acc.at[0], out_ref, out_sem)
        done.start()
        for t in (6, 7):
            core_copy(t).wait_send()
        for color in range(3):
            for bits in range(1, 8):
                chip_copy(color, stage_of(color, bits), bits).wait_send()
        done.wait()


def head_back(z, emb, stats, labels, parts, vocab, inv_n, collective_id):
    n, padded = z.shape
    d = emb.shape[1]
    rows = n // 16
    half = rows // 2

    def block(i):
        return (device_of(moved(my_place(), 7 - i // 4, 1 - (i // 2) % 2)) * 2 + i % 2, 0)

    return pl.pallas_call(
        functools.partial(back_kernel, make_chunks(padded), vocab, inv_n, parts, half),
        grid=(32,),
        in_specs=[pl.BlockSpec((half, padded), block),
                  pl.BlockSpec((padded, d), lambda i: (0, 0), pipeline_mode=pl.Buffered(1)),
                  pl.BlockSpec((half, 2), block),
                  pl.BlockSpec((half, 1), block)],
        out_specs=[pl.BlockSpec((half, padded), block), ANY],
        out_shape=[jax.ShapeDtypeStruct((n, padded), BF), jax.ShapeDtypeStruct((rows, d), F32)],
        scratch_shapes=[pltpu.VMEM((10, rows, d), F32), pltpu.VMEM((8, rows, d), F32), pltpu.VMEM((7, rows, d), F32),
                        DMA((8,)), DMA((8,)),
                        DMA((24,)), DMA((24,)), DMA],
        compiler_params=pltpu.CompilerParams(collective_id=collective_id, has_side_effects=True, vmem_limit_bytes=VMEM_LIMIT,
                                             ),
        name="head_back",
    )(z, emb, stats, labels)


def tail_kernel(chunks, vocab, views, swap_rows, dz_ref, hn_ref, *refs):
    n_in = max(v[0] for v in views) + 2
    ins, rows_ref = refs[:n_in - 1], refs[n_in - 1]
    de_ref = refs[n_in]
    outs = refs[n_in + 1:n_in + 4]
    back_ref = refs[n_in + 4]
    rest = refs[n_in + 5:]
    accs, pairs, boxes = rest[0:3], rest[3:6], rest[6:9]
    (load_sem, core_send, core_recv, send_sem, recv_sem, out_sem, sp_send, sp_recv, row_send, row_recv, row_sem) = rest[9:]
    i = pl.program_id(0)
    me = my_place()

    def source(color, place):
        which, rows, start, col, cols = views[color]
        m, f = mesh_id(place)
        return ins[which].at[pl.ds(pl.multiple_of(start(m, f), 8), rows), pl.ds(col, cols)]

    def load(color, bits):
        return pltpu.make_async_copy(source(color, flipped(me, bits)), accs[color].at[bits], load_sem.at[color * 8 + bits])

    def core_copy(color, bits):
        k = color * 8 + bits
        return pltpu.make_async_remote_copy(
            src_ref=source(color, flipped(me, bits, True)), dst_ref=pairs[color].at[bits],
            send_sem=core_send.at[k], recv_sem=core_recv.at[k],
            device_id=mesh_id(flipped(me, 0, True)), device_id_type=MESH)

    def chip_copy(color, stage, bits):
        slot = box_slot(color, stage, bits & ~ORDERS[color][stage])
        k = color * 8 + slot
        return pltpu.make_async_remote_copy(
            src_ref=accs[color].at[bits], dst_ref=boxes[color].at[slot],
            send_sem=send_sem.at[k], recv_sem=recv_sem.at[k],
            device_id=mesh_id(flipped(me, ORDERS[color][stage])), device_id_type=MESH)

    def row_copy(bits, core):
        k = 2 * bits + int(core)
        peer = flipped(me, bits, core)
        return pltpu.make_async_remote_copy(
            src_ref=rows_ref.at[pl.ds(pl.multiple_of(device_of(peer) * swap_rows, 8), swap_rows)],
            dst_ref=back_ref.at[pl.ds(pl.multiple_of(device_of(me) * swap_rows, 8), swap_rows)],
            send_sem=row_send.at[k], recv_sem=row_recv.at[k], device_id=mesh_id(peer), device_id_type=MESH)

    def row_arrival(bits, core):
        k = 2 * bits + int(core)
        peer = flipped(me, bits, core)
        dst = back_ref.at[pl.ds(pl.multiple_of(device_of(peer) * swap_rows, 8), swap_rows)]
        return pltpu.make_async_remote_copy(
            src_ref=dst, dst_ref=dst, send_sem=row_send.at[k], recv_sem=row_recv.at[k],
            device_id=mesh_id(peer), device_id_type=MESH)

    own_rows = pl.ds(pl.multiple_of(device_of(me) * swap_rows, 8), swap_rows)
    row_local = pltpu.make_async_copy(rows_ref.at[own_rows], back_ref.at[own_rows], row_sem)
    others = [(b, c) for b in BLOCK_ORDER for c in (False, True) if b or c]

    halves = ((2, 4), (4, 2))

    def target(color, place, half):
        rows = views[color][1]
        m, f = mesh_id(place)
        return outs[color].at[pl.ds(pl.multiple_of(m * rows + half * (rows // 2), 8), rows // 2)]

    def spread_copy(color, half, step, bits):
        rows = views[color][1]
        first, second = halves[half]
        src = accs[color].at[0, pl.ds(half * (rows // 2), rows // 2)] if bits == 0 else target(color, flipped(me, bits), half)
        k = (color * 2 + half) * 3 + step
        return pltpu.make_async_remote_copy(
            src_ref=src, dst_ref=target(color, flipped(me, bits), half),
            send_sem=sp_send.at[k], recv_sem=sp_recv.at[k],
            device_id=mesh_id(flipped(me, first if step == 0 else second)), device_id_type=MESH)

    def out_copy(color):
        rows = views[color][1]
        m, f = mesh_id(me)
        return pltpu.make_async_copy(accs[color].at[0], outs[color].at[pl.ds(pl.multiple_of(m * rows, 8), rows)], out_sem.at[color])

    @pl.when(i == 0)
    def _():
        barrier = pltpu.get_barrier_semaphore()
        for bits, core in others:
            pl.semaphore_signal(barrier, inc=1, device_id=mesh_id(flipped(me, bits, core)), device_id_type=MESH)
        pl.semaphore_wait(barrier, len(others))
        for bits in BLOCK_ORDER:
            for color in range(3):
                core_copy(color, bits).start()
                load(color, bits).start()
        row_local.start()
        de_ref[...] = jnp.zeros_like(de_ref)

    hn = hn_ref[...]
    for lo, count in chunks:
        keep = min(count, vocab - lo)
        part = lax.dot_general(dz_ref[:, lo:lo + count], hn, TN, preferred_element_type=F32)
        de_ref[lo:lo + keep, :] += part[:keep]

    for t in range(8):
        bits = BLOCK_ORDER[t]

        @pl.when(i == t)
        def _(bits=bits):
            for color in range(3):
                rows = views[color][1]
                load(color, bits).wait()
                core_copy(color, bits).wait_recv()
                add_rows(accs[color], bits, pairs[color], bits, 0, rows, 8)
                if stage_of(color, bits) == 0:
                    chip_copy(color, 0, bits).start()

    @pl.when(i == 8)
    def _():
        for bits, core in others:
            row_copy(bits, core).start()

    def arrivals(stage, index):
        for color in range(3):
            order = ORDERS[color]
            bits = sorted(subsets(order[stage + 1:]), key=lambda b: stage_of(color, b))[index]
            slot = box_slot(color, stage, bits)
            chip_copy(color, stage, bits | order[stage]).wait_recv()
            add_rows(accs[color], bits, boxes[color], slot, 0, views[color][1], 8)
            if stage_of(color, bits) == stage + 1 and stage < 2:
                chip_copy(color, stage + 1, bits).start()

    for step, (stage, index) in enumerate([(s, j) for s in range(2) for j in range(4 >> s)]):
        @pl.when(i == 9 + step)
        def _(stage=stage, index=index):
            arrivals(stage, index)

    @pl.when(i == 15)
    def _():
        arrivals(2, 0)
        for color in range(3):
            out_copy(color).start()
            for half in range(2):
                for step in range(2):
                    spread_copy(color, half, step, 0).start()
        for color in range(3):
            for half in range(2):
                spread_copy(color, half, 0, halves[half][0]).wait_recv()
                spread_copy(color, half, 2, halves[half][0]).start()
        for bits, core in others:
            row_arrival(bits, core).wait_recv()
        for color in range(3):
            for half in range(2):
                first, second = halves[half]
                spread_copy(color, half, 1, second).wait_recv()
                spread_copy(color, half, 2, first | second).wait_recv()
        for color in range(3):
            for bits in range(8):
                core_copy(color, bits).wait_send()
                if bits:
                    chip_copy(color, stage_of(color, bits), bits).wait_send()
            for half in range(2):
                for step in range(3):
                    spread_copy(color, half, step, halves[half][0] if step == 2 else 0).wait_send()
            out_copy(color).wait()
        for bits, core in others:
            row_copy(bits, core).wait_send()
        row_local.wait()


def tail_all(dz, hn, arrays, rows, views, piece_shapes, vocab, swap_rows, collective_id):
    n, padded = dz.shape
    d = hn.shape[1]
    block = n // 16
    scratch = []
    for count in (8, 8, 7):
        for shape in piece_shapes:
            scratch.append(pltpu.VMEM((count,) + shape, F32))
    sems = [DMA((24,))] * 5 + [DMA((3,))] + [DMA((18,))] * 2 + [DMA((16,))] * 2 + [DMA]
    return pl.pallas_call(
        functools.partial(tail_kernel, make_chunks(padded), vocab, views, swap_rows),
        grid=(16,),
        in_specs=[pl.BlockSpec((block, padded), lambda i: (i, 0)), pl.BlockSpec((block, d), lambda i: (i, 0))]
        + [ANY] * (len(arrays) + 1),
        out_specs=[pl.BlockSpec((vocab, d), lambda i: (0, 0), pipeline_mode=pl.Buffered(1))] + [ANY] * 4,
        out_shape=[jax.ShapeDtypeStruct((vocab, d), F32)]
        + [jax.ShapeDtypeStruct((4 * r, c), F32) for r, c in piece_shapes]
        + [jax.ShapeDtypeStruct(rows.shape, F32)],
        scratch_shapes=scratch + sems,
        compiler_params=pltpu.CompilerParams(collective_id=collective_id, has_side_effects=True, vmem_limit_bytes=VMEM_LIMIT,
                                             ),
        name="tail_all",
    )(dz, hn, *arrays, rows)


def moved(place, bits, core):
    x, y, z, c = place
    flips = (bits % 2, (bits // 2) % 2, bits // 4, core)
    return tuple(p + q - 2 * p * q for p, q in zip((x, y, z, c), flips))


ARRIVALS = {1: ((0, 0), (1, 0), (2, 0)), 2: ((1, 1),), 3: ((2, 1),), 4: ((2, 2),), 7: ((2, 3),)}


def logits_kernel(chunks, vocab, parts, rows, in_ref, emb_ref, lab_ref, all_ref, z_ref, st_ref, blocks, load_sem, *sems):
    i = pl.program_id(0)
    me = my_place()
    g = Gather(me, parts, rows, in_ref, all_ref, *sems)

    def load(step):
        at = device_of(moved(me, step // 2, step % 2)) * rows
        return pltpu.make_async_copy(all_ref.at[pl.ds(pl.multiple_of(at, CHUNK), rows)], blocks.at[step % 2], load_sem.at[step % 2])

    first = pltpu.make_async_copy(in_ref, blocks.at[0], load_sem.at[0])

    @pl.when(i == 0)
    def _():
        g.begin()
        first.start()

    for step, groups in ARRIVALS.items():
        @pl.when(i == step)
        def _(groups=groups):
            for stage, index in groups:
                g.arrive(stage, index)

    for bits in range(8):
        @pl.when(i == 2 * bits)
        def _(bits=bits):
            g.core_arrive(bits)

    @pl.when(i < 15)
    def _():
        load(i + 1).start()

    load(i).wait()
    hn = blocks[i % 2]
    lab = lab_ref[...]
    top = lab_z = total = None
    for lo, count in chunks:
        z = lax.dot_general(hn, emb_ref[lo:lo + count, :], NT, preferred_element_type=F32)
        z_ref[:, lo:lo + count] = z
        col = lax.broadcasted_iota(jnp.int32, z.shape, 1) + lo
        picked = jnp.sum(jnp.where(col == lab, z, 0.0), axis=1, keepdims=True)
        if lo + count > vocab:
            z = jnp.where(col < vocab, z, -jnp.inf)
        peak = jnp.max(z, axis=1, keepdims=True)
        top = peak if top is None else jnp.maximum(top, peak)
        lab_z = picked if lab_z is None else lab_z + picked
    for lo, count in chunks:
        z = z_ref[:, lo:lo + count]
        e = jnp.exp(z - top)
        if lo + count > vocab:
            col = lax.broadcasted_iota(jnp.int32, z.shape, 1) + lo
            e = jnp.where(col < vocab, e, 0.0)
        part = jnp.sum(e, axis=1, keepdims=True)
        total = part if total is None else total + part
    lane = lax.broadcasted_iota(jnp.int32, (rows, 128), 1)
    packed = jnp.where(lane == 0, top, jnp.where(lane == 1, total, lab_z))
    st_ref[...] = packed.T[:CHUNK]

    @pl.when(i == 15)
    def _():
        g.finish()


def make_chunks(padded):
    units = padded // 128
    count = (units + 7) // 8
    out, lo = [], 0
    for k in range(count, 0, -1):
        take = min(units, ((units + k - 1) // k + 1) // 2 * 2)
        out.append((lo, take * 128))
        lo += take * 128
        units -= take
    return tuple(out)


def head_logits(hn, emb, labels, parts, vocab, collective_id):
    rows, d = hn.shape
    n = 16 * rows
    padded = emb.shape[0]

    def block(i):
        return (device_of(moved(my_place(), i // 2, i % 2)), 0)

    return pl.pallas_call(
        functools.partial(logits_kernel, make_chunks(padded), vocab, parts, rows),
        grid=(16,),
        in_specs=[ANY, pl.BlockSpec((padded, d), lambda i: (0, 0), pipeline_mode=pl.Buffered(1)), pl.BlockSpec((rows, 1), block)],
        out_specs=[ANY, pl.BlockSpec((rows, padded), block), pl.BlockSpec((CHUNK, rows), block)],
        out_shape=[jax.ShapeDtypeStruct((n, d), BF), jax.ShapeDtypeStruct((n, padded), F32),
                   jax.ShapeDtypeStruct((16 * CHUNK, rows), F32)],
        scratch_shapes=[pltpu.VMEM((2, rows, d), BF), DMA((2,))] + gather_sems(),
        compiler_params=pltpu.CompilerParams(collective_id=collective_id, has_side_effects=True, vmem_limit_bytes=VMEM_LIMIT),
        name="head_logits",
    )(hn, emb, labels)


def mlp_forward(x_emb, gain_in, w_in, w_down):
    normed_in, norm_in_back = jax.vjp(lambda values: rms_scale(values, gain_in), x_emb)
    normed_bf = normed_in.astype(BF)
    both = jnp.dot(normed_bf, w_in, preferred_element_type=F32).astype(BF)
    hidden = w_down.shape[0]
    gate_f = both[:, :hidden].astype(F32)
    up_f = both[:, hidden:].astype(F32)
    gate_sig = jax.nn.sigmoid(gate_f)
    silu_gate = gate_f * gate_sig
    act_bf = (silu_gate * up_f).astype(BF)
    mlp_out = jnp.dot(act_bf, w_down, preferred_element_type=F32).astype(BF)
    h_res = x_emb + mlp_out.astype(F32)
    return h_res, (norm_in_back, normed_bf, gate_f, up_f, gate_sig, silu_gate, act_bf)


def mlp_backward(d_hidden, saved, w_in, w_down):
    norm_in_back, normed_bf, gate_f, up_f, gate_sig, silu_gate, act_bf = saved
    d_mlp = d_hidden.astype(BF)
    d_act = jnp.einsum("td,fd->tf", d_mlp, w_down, preferred_element_type=F32)
    grad_down = jnp.einsum("tf,td->fd", act_bf, d_mlp, preferred_element_type=F32)
    d_gate = (d_act * up_f * (gate_sig * (1.0 + gate_f * (1.0 - gate_sig)))).astype(BF)
    d_up = (d_act * silu_gate).astype(BF)
    d_both = jnp.concatenate([d_gate, d_up], axis=1)
    grad_in = jnp.einsum("td,tf->df", normed_bf, d_both, preferred_element_type=F32)
    d_normed = jnp.einsum("tf,df->td", d_both, w_in, preferred_element_type=F32)
    d_x = d_hidden + norm_in_back(d_normed)[0]
    return d_x, grad_in, grad_down


HN_PARTS = ((0, 176), (176, 176), (352, 160))
STAT_PARTS = ((0, 8), (8, 8), (16, 8))


def solution(mesh):
    tok_spec = P("fsdp")
    row_spec = P(AXES)
    weight_spec = P("fsdp")

    def device_step(tok_ids, tok_labels, table_shard, gate_shard, up_shard, down_shard, gain_in, gain_out):
        m_idx = lax.axis_index("model")
        f_idx = lax.axis_index("fsdp")
        me = m_idx * 4 + f_idx
        vocab, width = table_shard.shape
        own = tok_ids.shape[0] * tok_ids.shape[1] // 4
        num_tokens = own * 16

        def full_weight(shard):
            rows = shard.shape[0] // 4
            piece = lax.dynamic_slice_in_dim(shard, m_idx * rows, rows, axis=0)
            return lax.all_gather(piece, ("fsdp", "model"), axis=0, tiled=True)

        w_in = full_weight(jnp.concatenate([gate_shard, up_shard], axis=1))
        w_down = full_weight(down_shard)
        tokens = lax.all_gather(jnp.stack([tok_ids.reshape(-1), tok_labels.reshape(-1)]), "fsdp", axis=0)
        tokens = tokens.reshape(4, 2, 4, own).transpose(1, 2, 0, 3).reshape(2, 16, own)
        ids, labels = tokens[0], tokens[1].reshape(num_tokens)
        my_ids = lax.dynamic_slice_in_dim(ids, me, 1, axis=0)[0]

        base = vocab * 16
        place = lax.broadcasted_iota(jnp.int32, ids.shape, 1)
        mine = (ids // vocab) == me
        owner = my_ids // vocab
        owner_hot = owner[None, :] == jnp.arange(16, dtype=jnp.int32)[:, None]
        keys = jnp.concatenate([
            jnp.where(mine, place, place + own) * base + ids,
            jnp.where(owner_hot, place, place + own) * base], axis=0)
        keys = lax.sort(keys, dimension=1)
        keys = jnp.pad(keys, ((0, 0), (0, ROUND_ROWS)), constant_values=own * base)
        rank = jnp.sum(jnp.where(owner_hot, jnp.cumsum(owner_hot.astype(jnp.int32), axis=1), 0), axis=0) - 1
        hot_all = (ids // vocab)[:, None, :] == jnp.arange(16, dtype=jnp.int32)[None, :, None]
        most = jnp.max(jnp.sum(hot_all.astype(jnp.int32), axis=2))
        rounds = (most + ROUND_ROWS - 1) // ROUND_ROWS

        def round_keys(first, r):
            key = lax.dynamic_slice(keys, (first, r * ROUND_ROWS), (16, ROUND_ROWS)).reshape(-1)
            return key < own * base, key

        def served(r):
            valid, key = round_keys(0, r)
            return valid, jnp.where(valid, key % base - me * vocab, 0)

        def returned(r):
            valid, key = round_keys(16, r)
            return jnp.where(valid, key // base, 0)

        def take_rows(values, rows):
            return jnp.take(values, rows, axis=0)

        def exchange(values):
            return lax.all_to_all(values, AXES, 0, 0, tiled=True)

        def lookup_round(state):
            r, x = state
            _, row = served(r)
            got = exchange(take_rows(table_shard, row))
            at = rank - r * ROUND_ROWS
            now = (at >= 0) & (at < ROUND_ROWS)
            fetched = take_rows(got, jnp.where(now, owner * ROUND_ROWS + at, 0))
            return r + 1, jnp.where(now[:, None], fetched, x)

        _, x_rows = lax.while_loop(lambda s: s[0] < rounds, lookup_round, (jnp.int32(0), jnp.zeros((own, width), BF)))
        x_emb = x_rows.astype(F32)

        h_res, saved = mlp_forward(x_emb, gain_in, w_in, w_down)
        hn_f, norm_out_back = jax.vjp(lambda values: rms_scale(values, gain_out), h_res)
        padded = (vocab + 127) // 128 * 128
        emb = jnp.pad(table_shard, ((0, padded - vocab), (0, 0)))
        loc_labels = labels - me * vocab
        in_here = (loc_labels >= 0) & (loc_labels < vocab)
        lab_col = jnp.where(in_here, loc_labels, -1).reshape(num_tokens, 1)
        hn_bf, z, local_stats = head_logits(hn_f.astype(BF), emb, lab_col, HN_PARTS, vocab, 0)
        packed = local_stats.reshape(16, CHUNK, own)[:, :3].transpose(1, 0, 2).reshape(24, num_tokens // 8)
        all_stats = gather_all(packed, STAT_PARTS, 1).reshape(16, 3, num_tokens)
        tops = all_stats[:, 0]
        row_max = jnp.max(tops, axis=0)
        sum_exp = jnp.sum(all_stats[:, 1] * jnp.exp(tops - row_max[None, :]), axis=0)
        label_logit = jnp.sum(all_stats[:, 2], axis=0)
        loss = jnp.sum(row_max + jnp.log(sum_exp) - label_logit) / num_tokens
        stat_cols = jnp.stack([row_max, sum_exp], axis=1)
        dz, d_hn = head_back(z, emb, stat_cols, lab_col, HN_PARTS, vocab, 1.0 / num_tokens, 2)
        d_hidden = norm_out_back(d_hn)[0]
        d_x, g_in, g_down = mlp_backward(d_hidden, saved, w_in, w_down)

        g_rows, hidden = w_in.shape[0] // 16, w_down.shape[0]
        d_rows = hidden // 16
        views = (
            (0, g_rows, lambda m, f: f * (4 * g_rows) + m * g_rows, 0, hidden),
            (0, g_rows, lambda m, f: f * (4 * g_rows) + m * g_rows, hidden, hidden),
            (1, d_rows, lambda m, f: f * (4 * d_rows) + m * d_rows, 0, width),
        )
        pieces = [(g_rows, hidden), (g_rows, hidden), (d_rows, width)]
        sent = take_rows(d_x, returned(0))
        d_head, grad_gate, grad_up, grad_down, got = tail_all(
            dz, hn_bf, [g_in, g_down], sent, views, pieces, vocab, ROUND_ROWS, 3)

        def add_round(grad, r, got):
            valid, row = served(r)
            return grad.at[row].add(jnp.where(valid[:, None], got, 0.0))

        def grad_round(state):
            r, grad = state
            return r + 1, add_round(grad, r, exchange(take_rows(d_x, returned(r))))

        _, grad_table = lax.while_loop(lambda s: s[0] < rounds, grad_round, (jnp.int32(1), add_round(d_head, 0, got)))
        return loss, grad_table, grad_gate, grad_up, grad_down

    return jax.shard_map(device_step, mesh=mesh, in_specs=(tok_spec, tok_spec, row_spec, weight_spec, weight_spec, weight_spec, P(), P()), out_specs=(P(), row_spec, weight_spec, weight_spec, weight_spec), check_vma=False)
```

time: 1260 us -> 683 us (0.54)
  waiting for transfers between devices: 713 us -> 56.3 us
  Pallas kernels: 0 us -> 442 us
  matrix products: 327 us -> 51.8 us
  other arithmetic: 139 us -> 43.5 us
  blocking collectives: 31.3 us -> 6.45 us
  local copies, waits for them, and re-layouts: 31.4 us -> 52.5 us
    pallas_call x0 -> x4, Pallas kernels: none -> 442 us  [the longest x1 200 us: tail_all(): pl.pallas_call(functools.partial(tail_kernel, make_chunks(padded), vocab,...]
    dot_general x12 -> x6, matrix products: 327 us -> 51.8 us  [the longest x1 11.3 us: mlp_forward(): both = jnp.dot(normed_bf, w_in, preferred_element_type=F32).astype(BF)]
    unnamed x11 -> x2, waiting for transfers between devices: 264 us -> 0.03 us
    psum x2 -> x0, waiting for transfers between devices: 205 us -> none  [the longest x1 129 us: device_step(): lax.psum(jnp.einsum('tv,vd->td', d_logits, table_part, preferred_element_...]
    all_gather x4 -> x2, waiting for transfers between devices: 194 us -> 24.8 us  [full_weight(): return lax.all_gather(piece, ('fsdp', 'model'), axis=0, tiled=True)]
    reduce_scatter x3 -> x0, waiting for transfers between devices: 50.3 us -> none  [the longest x1 50.2 us: device_step(): lax.psum_scatter(grad_down, 'fsdp', scatter_dimension=0, tiled=True)]
    convert_element_type x1 -> x2, other arithmetic: 50.2 us -> 1.08 us  [the longest x1 1.08 us: device_step(): hn_f.astype(BF)]
    all_to_all x0 -> x1, waiting for transfers between devices: none -> 31.5 us  [exchange(): return lax.all_to_all(values, AXES, 0, 0, tiled=True)]
  transfers between devices with their start and end apart: 10 -> 3, of which waited for: 8 -> 2; matrix products, arithmetic and copies ran while one was open for 17% -> 7% of each run, Pallas kernels for 0% -> 0%
where the time goes in v2:
time: 683 us; the launch traced here: 676 us
  Pallas kernels  442 us (65%)
  waiting for transfers between devices  56.3 us (8%)
  local copies, waits for them, and re-layouts  52.5 us (8%)
  matrix products  51.8 us (8%)
  other arithmetic  43.5 us (6%)
  between operations  18.8 us (3%)
    pallas_call x1, Pallas kernels, tail_all(): pl.pallas_call(functools.partial(tail_kernel, make_chunks(padded), vocab,...  200 us
    pallas_call x1, Pallas kernels, head_back(): pl.pallas_call(functools.partial(back_kernel, make_chunks(padded), vocab,...  131 us
    pallas_call x1, Pallas kernels, head_logits(): pl.pallas_call(functools.partial(logits_kernel, make_chunks(padded), voca...  99.5 us
    all_to_all x1, waiting for transfers between devices, exchange(): return lax.all_to_all(values, AXES, 0, 0, tiled=True)  31.5 us
    all_gather x2, waiting for transfers between devices, full_weight(): return lax.all_gather(piece, ('fsdp', 'model'), axis=0, tiled=True)  24.8 us
    scatter-add x1, other arithmetic, add_round(): return grad.at[row].add(jnp.where(valid[:, None], got, 0.0))  18.1 us
    unnamed x44, local copies, waits for them, and re-layouts  16.8 us
  transfers between devices with their start and end apart: 3, of which 2 were waited for; matrix products, arithmetic and copies ran while one was open for 7% of the time, Pallas kernels for 0%

profile of v2, /device:TPU:0, one launch (start us, length us, event | category | flops | bytes accessed | tf_op | source)
XLA Modules:
  0.0 676.2 jit_solution(14875428314948390531)
XLA Ops:
  8.1 0.7 add_bitcast_fusion
  8.8 6.4 all-gather.1
  15.5 0.6 pad_add_fusion
  16.2 1.9 fusion.32
  18.2 1.7 constant_dynamic-slice_fusion
  19.9 0.4 convert_reduce_fusion
  20.3 0.6 reduce_max.18
  21.6 1.2 reduce-window.6
  22.8 0.2 slice_reduce_fusion.1
  23.0 0.1 select_reduce_fusion
  23.1 5.3 sub.176
  28.4 4.7 and_select_fusion.2.lab_ref
  33.1 4.9 pad.9.emb_ref
  38.1 0.7 slice_compare_fusion
  38.9 0.1 lt.313
  39.0 0.1 and.191
  39.1 0.1 and.193
  39.2 0.7 lt.319
  40.0 0.7 slice_remainder_fusion
  41.0 0.8 pad.8
  41.8 0.6 pad_clamp_fusion.3
  42.4 0.6 fusion.48
  43.1 47.2 %while.24 = (s32[]{:T(128)}, bf16[512,768]{1,0:T(8,128)(2,1)S(1)}, s32[]{:T(128)}, s32[512]{0:T(512)S(1)}, s32[512]{0:T(512)S(1)}, /*index=5*/s32[32,568]{1,0:T(...) while((s32[]{:T(128)}, bf16[512,768]{1,0:T(8,128)(2,1)S(1)}, ...), condition=%wide.region_7.8_spmd, body=%wide.region_6.7_spmd.sunk | while | flops 1507206 | bytes 13624787 | solution.py:690
  43.5 7.5 %gather_fusion = bf16[896,768]{1,0:T(8,128)(2,1)S(1)} fusion(bf16[3144,768]{1,0:T(8,128)(2,1)} %get-tuple-element.423, s32[1024]{0:T(1024)S(1)} %pad_clamp_fusion.7), kind=kCustom, calls=%fused_computation.clone.1 | custom fusion | bytes 2756096 | tf_op jit(solution)/shard_map/while/body/jit(_take)/gather | solution.py:676
  51.0 1.3 broadcast_select_fusion.5
  52.3 4.1 all-to-all-start
  56.4 31.5 %all-to-all-done = bf16[16,56,768]{2,1,0:T(8,128)(2,1)S(1)} async-done(((bf16[16,56,768]{2,1,0:T(8,128)(2,1)}), bf16[16,56,768]{2,1,0:T(8,128)(2,1)S(1)}, u32[]{:S(2)}, u32[]{:S(2)}) %all-to-all-start) | async-done | bytes 1376288 | tf_op jit(solution)/shard_map/while/body/all_to_all | solution.py:679
  87.9 2.0 gather_fusion.1
  89.9 0.3 select_select_fusion.2
  90.3 0.2 fusion.25
  90.6 11.3 %convolution_convert_fusion = bf16[512,6144]{1,0:T(8,128)(2,1)} fusion(bf16[768,6144]{1,0:T(8,128)(2,1)} %all-gather.5.cloned.1.call-done, bf16[512,768]{1,0:T(8,128)(2,1)S(1)} %get-tuple-element.207, f32[768]{0:T(1024)S(1)} %copy-done.11, f32[512]{0:T(512)S(1)} %fusion.52), kind=kOutput, calls=%fused_computation.53 | convolution fusion | flops 4836556800 | bytes 16520192 | tf_op jit(solution)/shard_map/dot_general | solution.py:593
  101.9 24.8 %all-gather.7.cloned.1.call-done = bf16[3072,768]{1,0:T(8,128)(2,1)} async-done(((bf16[192,768]{1,0:T(8,128)(2,1)}), bf16[3072,768]{1,0:T(8,128)(2,1)}) %all-gather.7.cloned.1.call-update) | async-done | bytes 4718608 | tf_op jit(solution)/shard_map/all_gather | solution.py:639
  126.7 7.4 %multiply_reduce_fusion.1 = (f32[512]{0:T(512)S(1)}, f32[512,768]{1,0:T(8,128)S(1)}) fusion(bf16[3072,768]{1,0:T(8,128)(2,1)} %all-gather.7.cloned.1.call-done, bf16[512,6144]{1,0:T(8,128)(2,1)} %convolution_convert_fusion, bf16[512,768]{1,0:T(8,128)(2,1)S(1)} %get-tuple-element.207), kind=kOutput, calls=%fused_computation.87 | convolution fusion | flops 2430860800 | bytes 13371392 | tf_op jit(solution)/shard_map/dot_general | solution.py:600
  134.1 1.1 copy-done.4
  135.2 1.1 multiply_convert_fusion.1.in_ref
  136.3 99.5 %head_logits.1 = (bf16[8192,768]{1,0:T(8,128)(2,1)}, f32[8192,3200]{1,0:T(8,128)}, f32[128,512]{1,0:T(8,128)}) custom-call(bf16[512,768]{1,0:T(8,128)(2,1)} %multiply_convert_fusion.1.in_ref, bf16[3200,768]{1,0:T(8,128)(2,1)} %pad.9.emb_ref, s32[8192,1]{1,0:T(8,128)} %and_select_fusion.2.lab_ref), custom_call_target="tpu_custom_call" | custom-call | tf_op jit(solution)/shard_map/head_logits/pallas_call | solution.py:577
  235.8 1.0 slice.57
  236.8 0.7 reshape.618.refs_0_
  237.5 12.3 %gather_stats.1 = f32[384,1024]{1,0:T(8,128)} custom-call(f32[24,1024]{1,0:T(8,128)} %reshape.618.refs_0_), custom_call_target="tpu_custom_call" | custom-call | tf_op jit(solution)/shard_map/gather_stats/pallas_call | solution.py:158
  249.8 2.8 reshape.619
  252.6 1.4 slice_reduce_fusion.2
  254.0 0.7 fusion.36
  254.7 0.6 subtract_reduce_fusion
  255.3 2.9 copy.37.st_ref
  258.3 130.8 %head_back.1 = (bf16[8192,3200]{1,0:T(8,128)(2,1)}, f32[512,768]{1,0:T(8,128)}) custom-call(f32[8192,3200]{1,0:T(8,128)} %get-tuple-element.209.z_ref, bf16[3200,768]{1,0:T(8,128)(2,1)} %pad.9.emb_ref, f32[8192,2]{1,0:T(8,128)} %copy.37.st_ref, s32[8192,1]{1,0:T(8,128)} %and_select_fusion.2.lab_ref), custom_call_target="tpu_custom_call" | custom-call | tf_op jit(solution)/shard_map/head_back/pallas_call | solution.py:281
  389.1 2.3 multiply_reduce_fusion
  391.4 0.5 copy-done.6
  391.9 0.3 add_add_fusion.1
  392.2 10.0 %fusion.37.refs_1_ = f32[3072,768]{1,0:T(8,128)} fusion(f32[512,768]{1,0:T(8,128)S(1)} %add_add_fusion.1, bf16[512,6144]{1,0:T(8,128)(2,1)} %convolution_convert_fusion), kind=kOutput, calls=%fused_computation.102 | convolution fusion | flops 2428895232 | bytes 17301504 | tf_op jit(solution)/shard_map/tf,td->fd/dot_general | solution.py:609
  402.2 5.0 fusion.14
  407.2 9.4 %fusion.21.refs_0_ = f32[768,6144]{1,0:T(8,128)} fusion(bf16[512,3072]{1,0:T(8,128)(2,1)S(1)} %get-tuple-element.265, bf16[512,3072]{1,0:T(8,128)(2,1)S(1)} %get-tuple-element.264, bf16[512,768]{1,0:T(8,128)(2,1)S(1)} %copy-done.3, f32[768]{0:T(1024)S(1)} %copy-done.11, f32[512]{0:T(512)S(1)} %fusion.52), kind=kOutput, calls=%fused_computation.68 | convolution fusion | flops 4845993984 | bytes 25957376 | tf_op jit(solution)/shard_map/td,tf->df/dot_general | solution.py:613
  416.7 8.8 %fusion.28 = (f32[512]{0:T(512)S(1)}, f32[512,768]{1,0:T(8,128)S(1)}) fusion(bf16[512,768]{1,0:T(8,128)(2,1)S(1)} %copy-done.3, f32[768]{0:T(1024)S(1)} %copy-done.11, bf16[768,6144]{1,0:T(8,128)(2,1)} %all-gather.5.cloned.1.call-done, bf16[512,3072]{1,0:T(8,128)(2,1)S(1)} %get-tuple-element.265, bf16[512,3072]{1,0:T(8,128)(2,1)S(1)} %get-tuple-element.264), kind=kOutput, calls=%fused_computation.84 | convolution fusion | flops 4845993472 | bytes 18093056 | tf_op jit(solution)/shard_map/tf,df->td/dot_general | solution.py:614
  425.5 0.4 fusion.24
  425.9 0.3 copy-done.13
  426.2 4.0 gather_fusion.3
  430.2 3.6 broadcast_select_fusion.2.refs_2_
  433.7 199.9 %tail_all.1 = (f32[3144,768]{1,0:T(8,128)}, f32[192,3072]{1,0:T(8,128)}, f32[192,3072]{1,0:T(8,128)}, f32[768,768]{1,0:T(8,128)}, f32[896,768]{1,0:T(8,128)}) custom-call(bf16[8192,3200]{1,0:T(8,128)(2,1)} %get-tuple-element.210.dz_ref, bf16[8192,768]{1,0:T(8,128)(2,1)} %get-tuple-element.211.hn_ref, f32[768,6144]{1,0:T(8,128)} %fusion.21.refs_0_, ...), custom_call_target="tpu_custom_call" | custom-call | tf_op jit(solution)/shard_map/tail_all/pallas_call | solution.py:470
  633.7 18.1 %scatter_custom_fusion.1 = f32[3144,768]{1,0:T(8,128)} fusion(f32[3144,768]{1,0:T(8,128)} %get-tuple-element.213, s32[896]{0:T(1024)} %fusion.48, f32[896,768]{1,0:T(8,128)} %get-tuple-element.214, f32[]{:T(128)} %constant.285.clone.1, pred[896]{0:T(1024)(128)(4,1)S(1)} %copy-done.14), kind=kCustom, calls=%fused_computation.74 | custom fusion | flops 1376256 | bytes 12412288 | tf_op jit(solution)/shard_map/scatter-add | solution.py:727
  652.4 8.3 %copy.74 = f32[3144,768]{1,0:T(8,128)} copy(f32[3144,768]{1,0:T(8,128)} %get-tuple-element.464) | data formatting | bytes 19316736
  660.7 1.4 copy.75
  662.1 1.1 copy-done.8
  663.2 1.4 copy.76
  664.6 1.1 copy-done.7
  665.8 1.4 copy.77
  (79 shorter events, 1.6 us)
Async XLA Ops:
  8.0 30.1 %sort.9.cloned.1.call-start = ((), (), s32[]{:S(2)}) async-start(), calls=%async_computation.4 | async-start | bytes 196640 | tf_op jit(solution)/shard_map/sort | solution.py:656
  16.2 74.4 %all-gather.5.cloned.1.call-start = ((), (), s32[]{:S(2)}) async-start(), calls=%async_computation.2 | async-start | bytes 10027008 | tf_op jit(solution)/shard_map/all_gather | solution.py:639
  18.2 108.5 %all-gather.7.cloned.1.call-start = ((), (), s32[]{:S(2)}) async-start(), calls=%async_computation.3 | async-start | bytes 5013504 | tf_op jit(solution)/shard_map/all_gather | solution.py:639
  43.1 47.5 %copy-start.11 = (f32[768]{0:T(1024)S(1)}, f32[768]{0:T(1024)}, u32[]{:S(2)}) copy-start(f32[768]{0:T(1024)} %param.18) | copy-start | bytes 9220
  52.3 35.6 %all-to-all-start = ((bf16[16,56,768]{2,1,0:T(8,128)(2,1)}), bf16[16,56,768]{2,1,0:T(8,128)(2,1)S(1)}, u32[]{:S(2)}, u32[]{:S(2)}) async-start(bf16[16,56,768]{2,1,0:T(8,128)(2,1)} %broadcast_select_fusion.5), calls=%async_computation | async-start | bytes 2752512 | tf_op jit(solution)/shard_map/while/body/all_to_all | solution.py:679
  90.3 11.6 %copy-start.10 = (s32[32,568]{1,0:T(8,128)}, s32[32,568]{1,0:T(8,128)S(1)}, u32[]{:S(2)}) copy-start(s32[32,568]{1,0:T(8,128)S(1)} %get-tuple-element.478) | copy-start | bytes 218116
  90.3 36.4 %copy-start.2 = (bf16[512,768]{1,0:T(8,128)(2,1)}, bf16[512,768]{1,0:T(8,128)(2,1)S(1)}, u32[]{:S(2)}) copy-start(bf16[512,768]{1,0:T(8,128)(2,1)S(1)} %get-tuple-element.207) | copy-start | bytes 2359300
  101.9 33.3 %copy-start.12 = (f32[768]{0:T(1024)S(1)}, f32[768]{0:T(1024)}, u32[]{:S(2)}) copy-start(f32[768]{0:T(1024)} %param.19) | copy-start | bytes 9220
  134.0 1.1 copy-start.4
  389.0 2.4 copy-start.5
  389.0 2.8 copy-start.6
  391.9 10.3 %slice-start = ((s8[4718592]{0:T(1024)(128)(4,1)}), s8[4194304]{0:T(1024)(128)(4,1)S(1)}, s32[]{:S(2)}) async-start(s8[4718592]{0:T(1024)(128)(4,1)} %bitcast.65), calls=%async_computation.6 | async-start | bytes 8388608
  391.9 10.3 %slice-start.2 = ((s8[6291456]{0:T(1024)(128)(4,1)}), s8[4194304]{0:T(1024)(128)(4,1)S(1)}, s32[]{:S(2)}) async-start(s8[6291456]{0:T(1024)(128)(4,1)} %bitcast.67), calls=%async_computation.8 | async-start | bytes 8388608
  392.2 10.0 %slice-start.1 = ((s8[4718592]{0:T(1024)(128)(4,1)}), s8[524288]{0:T(1024)(128)(4,1)S(1)}, s32[]{:S(2)}) async-start(s8[4718592]{0:T(1024)(128)(4,1)} %bitcast.65), calls=%async_computation.7 | async-start | bytes 1048576
  392.2 10.0 %slice-start.3 = ((s8[6291456]{0:T(1024)(128)(4,1)}), s8[2097152]{0:T(1024)(128)(4,1)S(1)}, s32[]{:S(2)}) async-start(s8[6291456]{0:T(1024)(128)(4,1)} %bitcast.67), calls=%async_computation.9 | async-start | bytes 4194304
  402.2 5.0 copy-start.3
  425.5 0.7 copy-start.13
  426.2 4.0 copy-start
  433.7 199.9 %copy-start.14 = (pred[896]{0:T(1024)(128)(4,1)S(1)}, pred[896]{0:T(1024)(128)(4,1)}, u32[]{:S(2)}) copy-start(pred[896]{0:T(1024)(128)(4,1)} %lt.319) | copy-start | bytes 2692
  633.7 18.1 %copy-start.1 = (f32[512,768]{1,0:T(8,128)S(1)}, f32[512,768]{1,0:T(8,128)}, u32[]{:S(2)}) copy-start(f32[512,768]{1,0:T(8,128)} %copy-done) | copy-start | bytes 4718596
  652.4 8.3 %copy-start.9 = (f32[192,3072]{1,0:T(8,128)S(1)}, f32[192,3072]{1,0:T(8,128)}, u32[]{:S(2)}) copy-start(f32[192,3072]{1,0:T(8,128)} %get-tuple-element.465) | copy-start | bytes 7077892
  660.7 2.5 copy-start.8
  663.2 2.5 copy-start.7
Sparse Core Ops, SparseCore 0:
  16.3 5.7 sort.11.cloned.1.call-done
  (1 shorter events, 0.0 us)
Sparse Core Ops, SparseCore 1:
  19.5 66.4 all-gather.4
  88.0 38.6 all-gather.6

commit v3 on v2

--- a/solution.py
+++ b/solution.py
@@ -219,15 +219,15 @@
 
     lab = lab_ref[...]
     top = st_ref[:, 0:1]
-    inv_sum = 1.0 / st_ref[:, 1:2]
+    scale = inv_n / st_ref[:, 1:2]
     total = None
     for lo, count in chunks:
         z = z_ref[:, lo:lo + count]
-        p = jnp.exp(z - top) * inv_sum
-        col = lax.broadcasted_iota(jnp.int32, z.shape, 1) + lo
-        p = jnp.where(col == lab, p - 1.0, p) * inv_n
+        p = jnp.exp(z - top) * scale
+        col = lax.broadcasted_iota(jnp.int32, z.shape, 1)
+        p = jnp.where(col == lab - lo, p - inv_n, p)
         if lo + count > vocab:
-            p = jnp.where(col < vocab, p, 0.0)
+            p = jnp.where(col < vocab - lo, p, 0.0)
         dz = p.astype(BF)
         dz_ref[:, lo:lo + count] = dz
         part = jnp.dot(dz, emb_ref[lo:lo + count, :], preferred_element_type=F32)
@@ -530,10 +530,10 @@
     for lo, count in chunks:
         z = lax.dot_general(hn, emb_ref[lo:lo + count, :], NT, preferred_element_type=F32)
         z_ref[:, lo:lo + count] = z
-        col = lax.broadcasted_iota(jnp.int32, z.shape, 1) + lo
-        picked = jnp.sum(jnp.where(col == lab, z, 0.0), axis=1, keepdims=True)
+        col = lax.broadcasted_iota(jnp.int32, z.shape, 1)
+        picked = jnp.sum(jnp.where(col == lab - lo, z, 0.0), axis=1, keepdims=True)
         if lo + count > vocab:
-            z = jnp.where(col < vocab, z, -jnp.inf)
+            z = jnp.where(col < vocab - lo, z, -jnp.inf)
         peak = jnp.max(z, axis=1, keepdims=True)
         top = peak if top is None else jnp.maximum(top, peak)
         lab_z = picked if lab_z is None else lab_z + picked
@@ -541,8 +541,8 @@
         z = z_ref[:, lo:lo + count]
         e = jnp.exp(z - top)
         if lo + count > vocab:
-            col = lax.broadcasted_iota(jnp.int32, z.shape, 1) + lo
-            e = jnp.where(col < vocab, e, 0.0)
+            col = lax.broadcasted_iota(jnp.int32, z.shape, 1)
+            e = jnp.where(col < vocab - lo, e, 0.0)
         part = jnp.sum(e, axis=1, keepdims=True)
         total = part if total is None else total + part
     lane = lax.broadcasted_iota(jnp.int32, (rows, 128), 1)
@@ -687,7 +687,7 @@
             fetched = take_rows(got, jnp.where(now, owner * ROUND_ROWS + at, 0))
             return r + 1, jnp.where(now[:, None], fetched, x)
 
-        _, x_rows = lax.while_loop(lambda s: s[0] < rounds, lookup_round, (jnp.int32(0), jnp.zeros((own, width), BF)))
+        _, x_rows = lax.while_loop(lambda s: s[0] < rounds, lookup_round, lookup_round((jnp.int32(0), jnp.zeros((own, width), BF))))
         x_emb = x_rows.astype(F32)
 
         h_res, saved = mlp_forward(x_emb, gain_in, w_in, w_down)

time: 683 us -> 680 us (level)
    all_to_all x1, waiting for transfers between devices: 31.5 us -> 20.9 us  [exchange(): return lax.all_to_all(values, AXES, 0, 0, tiled=True)]
    unnamed x44 -> x50, local copies, waits for them, and re-layouts: 16.8 us -> 16.9 us
  transfers between devices with their start and end apart: 3 -> 3, of which waited for: 2 -> 3; matrix products, arithmetic and copies ran while one was open for 7% -> 7% of each run, Pallas kernels for 0% -> 0%
where the time goes in v3:
time: 680 us; the launch traced here: 672 us
  Pallas kernels  444 us (65%)
  waiting for transfers between devices  52.3 us (8%)
  local copies, waits for them, and re-layouts  51.5 us (8%)
  matrix products  51.4 us (8%)
  other arithmetic  43 us (6%)
  between operations  18.9 us (3%)
    pallas_call x1, Pallas kernels, tail_all(): pl.pallas_call(functools.partial(tail_kernel, make_chunks(padded), vocab,...  200 us
    pallas_call x1, Pallas kernels, head_back(): pl.pallas_call(functools.partial(back_kernel, make_chunks(padded), vocab,...  131 us
    pallas_call x1, Pallas kernels, head_logits(): pl.pallas_call(functools.partial(logits_kernel, make_chunks(padded), voca...  101 us
    all_gather x2, waiting for transfers between devices, full_weight(): return lax.all_gather(piece, ('fsdp', 'model'), axis=0, tiled=True)  31.3 us
    all_to_all x1, waiting for transfers between devices, exchange(): return lax.all_to_all(values, AXES, 0, 0, tiled=True)  20.9 us
    scatter-add x1, other arithmetic, add_round(): return grad.at[row].add(jnp.where(valid[:, None], got, 0.0))  17.8 us
    unnamed x50, local copies, waits for them, and re-layouts  16.9 us
  transfers between devices with their start and end apart: 3, of which 3 were waited for; matrix products, arithmetic and copies ran while one was open for 7% of the time, Pallas kernels for 0%

profile of v3, /device:TPU:0, one launch (start us, length us, event | category | flops | bytes accessed | tf_op | source)
XLA Modules:
  0.0 671.8 jit_solution(8396884590887996618)
XLA Ops:
  8.1 0.7 add_bitcast_fusion
  8.8 6.4 all-gather.1
  15.5 0.6 pad_add_fusion
  16.2 1.9 fusion.32
  18.2 1.7 constant_dynamic-slice_fusion
  20.0 1.2 reduce-window.6
  21.1 0.2 slice_reduce_fusion.1
  21.4 0.1 select_reduce_fusion
  21.5 5.3 sub.193
  26.7 4.7 and_select_fusion.2.lab_ref
  31.4 0.7 fusion.47
  32.3 0.7 slice_divide_fusion
  33.2 7.5 %gather_fusion.3 = bf16[896,768]{1,0:T(8,128)(2,1)S(1)} fusion(bf16[3144,768]{1,0:T(8,128)(2,1)} %param.14, s32[1024]{0:T(1024)S(1)} %pad_clamp_fusion.5), kind=kCustom, calls=%fused_computation.3 | custom fusion | bytes 2756096 | tf_op jit(solution)/shard_map/jit(_take)/gather | solution.py:676
  40.7 1.3 broadcast_select_fusion.3
  41.9 4.1 all-to-all-start.2
  46.1 0.4 convert_reduce_fusion
  46.4 0.6 reduce_max.18
  47.7 5.0 pad.9.emb_ref
  52.7 0.7 lt.376
  53.5 0.1 lt.374
  53.6 0.1 and.248
  53.7 0.1 and.250
  54.0 0.6 pad_clamp_fusion.3
  54.6 0.6 compare_and_fusion.6
  55.2 20.9 %all-to-all-done.2 = bf16[16,56,768]{2,1,0:T(8,128)(2,1)S(1)} async-done(((bf16[16,56,768]{2,1,0:T(8,128)(2,1)}), bf16[16,56,768]{2,1,0:T(8,128)(2,1)S(1)}, u32[]{:S(2)}, u32[]{:S(2)}) %all-to-all-start.2) | async-done | bytes 1376288 | tf_op jit(solution)/shard_map/all_to_all | solution.py:679
  76.2 2.0 gather_fusion.4
  78.2 0.2 select_select_fusion.1
  78.4 0.5 while.24
  78.9 0.2 fusion.25
  79.2 3.5 all-gather.5.cloned.1.call-done
  82.7 10.8 %convolution_convert_fusion = bf16[512,6144]{1,0:T(8,128)(2,1)} fusion(bf16[768,6144]{1,0:T(8,128)(2,1)} %all-gather.5.cloned.1.call-done, bf16[512,768]{1,0:T(8,128)(2,1)S(1)} %get-tuple-element.207, f32[768]{0:T(1024)S(1)} %copy-done.12, f32[512]{0:T(512)S(1)} %fusion.56), kind=kOutput, calls=%fused_computation.55 | convolution fusion | flops 4836556800 | bytes 16520192 | tf_op jit(solution)/shard_map/dot_general | solution.py:593
  93.4 27.8 %all-gather.7.cloned.1.call-done = bf16[3072,768]{1,0:T(8,128)(2,1)} async-done(((bf16[192,768]{1,0:T(8,128)(2,1)}), bf16[3072,768]{1,0:T(8,128)(2,1)}) %all-gather.7.cloned.1.call-update) | async-done | bytes 4718608 | tf_op jit(solution)/shard_map/all_gather | solution.py:639
  121.3 7.4 %multiply_reduce_fusion.1 = (f32[512]{0:T(512)S(1)}, f32[512,768]{1,0:T(8,128)S(1)}) fusion(bf16[3072,768]{1,0:T(8,128)(2,1)} %all-gather.7.cloned.1.call-done, bf16[512,6144]{1,0:T(8,128)(2,1)} %convolution_convert_fusion, bf16[512,768]{1,0:T(8,128)(2,1)S(1)} %get-tuple-element.207), kind=kOutput, calls=%fused_computation.89 | convolution fusion | flops 2430860800 | bytes 13371392 | tf_op jit(solution)/shard_map/dot_general | solution.py:600
  128.7 1.1 copy-done.4
  129.8 1.1 multiply_convert_fusion.1.in_ref
  130.9 100.5 %head_logits.1 = (bf16[8192,768]{1,0:T(8,128)(2,1)}, f32[8192,3200]{1,0:T(8,128)}, f32[128,512]{1,0:T(8,128)}) custom-call(bf16[512,768]{1,0:T(8,128)(2,1)} %multiply_convert_fusion.1.in_ref, bf16[3200,768]{1,0:T(8,128)(2,1)} %pad.9.emb_ref, s32[8192,1]{1,0:T(8,128)} %and_select_fusion.2.lab_ref), custom_call_target="tpu_custom_call" | custom-call | tf_op jit(solution)/shard_map/head_logits/pallas_call | solution.py:577
  231.4 1.0 slice.61
  232.4 0.7 reshape.736.refs_0_
  233.1 12.3 %gather_stats.1 = f32[384,1024]{1,0:T(8,128)} custom-call(f32[24,1024]{1,0:T(8,128)} %reshape.736.refs_0_), custom_call_target="tpu_custom_call" | custom-call | tf_op jit(solution)/shard_map/gather_stats/pallas_call | solution.py:158
  245.4 3.0 reshape.737
  248.4 1.4 slice_reduce_fusion.2
  249.8 0.7 fusion.36
  250.5 0.6 subtract_reduce_fusion
  251.2 2.7 copy.37.st_ref
  253.9 130.7 %head_back.1 = (bf16[8192,3200]{1,0:T(8,128)(2,1)}, f32[512,768]{1,0:T(8,128)}) custom-call(f32[8192,3200]{1,0:T(8,128)} %get-tuple-element.209.z_ref, bf16[3200,768]{1,0:T(8,128)(2,1)} %pad.9.emb_ref, f32[8192,2]{1,0:T(8,128)} %copy.37.st_ref, s32[8192,1]{1,0:T(8,128)} %and_select_fusion.2.lab_ref), custom_call_target="tpu_custom_call" | custom-call | tf_op jit(solution)/shard_map/head_back/pallas_call | solution.py:281
  384.6 2.3 multiply_reduce_fusion
  386.9 0.5 copy-done.6
  387.4 0.3 add_add_fusion.1
  387.8 9.9 %fusion.37.refs_1_ = f32[3072,768]{1,0:T(8,128)} fusion(f32[512,768]{1,0:T(8,128)S(1)} %add_add_fusion.1, bf16[512,6144]{1,0:T(8,128)(2,1)} %convolution_convert_fusion), kind=kOutput, calls=%fused_computation.106 | convolution fusion | flops 2428895232 | bytes 17301504 | tf_op jit(solution)/shard_map/tf,td->fd/dot_general | solution.py:609
  397.8 5.0 fusion.14
  402.8 9.5 %fusion.21.refs_0_ = f32[768,6144]{1,0:T(8,128)} fusion(bf16[512,3072]{1,0:T(8,128)(2,1)S(1)} %get-tuple-element.269, bf16[512,3072]{1,0:T(8,128)(2,1)S(1)} %get-tuple-element.268, bf16[512,768]{1,0:T(8,128)(2,1)S(1)} %copy-done.3, f32[768]{0:T(1024)S(1)} %copy-done.12, f32[512]{0:T(512)S(1)} %fusion.56), kind=kOutput, calls=%fused_computation.70 | convolution fusion | flops 4845993984 | bytes 25957376 | tf_op jit(solution)/shard_map/td,tf->df/dot_general | solution.py:613
  412.2 8.8 %fusion.28 = (f32[512]{0:T(512)S(1)}, f32[512,768]{1,0:T(8,128)S(1)}) fusion(bf16[512,768]{1,0:T(8,128)(2,1)S(1)} %copy-done.3, f32[768]{0:T(1024)S(1)} %copy-done.12, bf16[768,6144]{1,0:T(8,128)(2,1)} %all-gather.5.cloned.1.call-done, bf16[512,3072]{1,0:T(8,128)(2,1)S(1)} %get-tuple-element.269, bf16[512,3072]{1,0:T(8,128)(2,1)S(1)} %get-tuple-element.268), kind=kOutput, calls=%fused_computation.86 | convolution fusion | flops 4845993472 | bytes 18093056 | tf_op jit(solution)/shard_map/tf,df->td/dot_general | solution.py:614
  421.1 0.4 fusion.24
  421.5 0.3 copy-done.14
  421.8 4.0 gather_fusion.5
  425.7 3.6 broadcast_select_fusion.2.refs_2_
  429.3 200.2 %tail_all.1 = (f32[3144,768]{1,0:T(8,128)}, f32[192,3072]{1,0:T(8,128)}, f32[192,3072]{1,0:T(8,128)}, f32[768,768]{1,0:T(8,128)}, f32[896,768]{1,0:T(8,128)}) custom-call(bf16[8192,3200]{1,0:T(8,128)(2,1)} %get-tuple-element.210.dz_ref, bf16[8192,768]{1,0:T(8,128)(2,1)} %get-tuple-element.211.hn_ref, f32[768,6144]{1,0:T(8,128)} %fusion.21.refs_0_, ...), custom_call_target="tpu_custom_call" | custom-call | tf_op jit(solution)/shard_map/tail_all/pallas_call | solution.py:470
  629.5 17.8 %scatter_custom_fusion.1 = f32[3144,768]{1,0:T(8,128)} fusion(f32[3144,768]{1,0:T(8,128)} %get-tuple-element.213, s32[896]{0:T(1024)} %copy-done.15, f32[896,768]{1,0:T(8,128)} %get-tuple-element.214, f32[]{:T(128)} %constant.318.clone.1, pred[896]{0:T(1024)(128)(4,1)S(1)} %copy-done.16), kind=kCustom, calls=%fused_computation.76 | custom fusion | flops 1376256 | bytes 12412288 | tf_op jit(solution)/shard_map/scatter-add | solution.py:727
  648.0 8.3 %copy.74 = f32[3144,768]{1,0:T(8,128)} copy(f32[3144,768]{1,0:T(8,128)} %get-tuple-element.472) | data formatting | bytes 19316736
  656.4 1.4 copy.75
  657.8 1.1 copy-done.8
  658.9 1.4 copy.76
  660.3 1.1 copy-done.7
  661.4 1.4 copy.77
  (79 shorter events, 1.3 us)
Async XLA Ops:
  8.0 23.4 %sort.9.cloned.1.call-start = ((), (), s32[]{:S(2)}) async-start(), calls=%async_computation.5 | async-start | bytes 196640 | tf_op jit(solution)/shard_map/sort | solution.py:656
  16.2 66.5 %all-gather.5.cloned.1.call-start = ((), (), s32[]{:S(2)}) async-start(), calls=%async_computation.3 | async-start | bytes 10027008 | tf_op jit(solution)/shard_map/all_gather | solution.py:639
  18.2 103.1 %all-gather.7.cloned.1.call-start = ((), (), s32[]{:S(2)}) async-start(), calls=%async_computation.4 | async-start | bytes 5013504 | tf_op jit(solution)/shard_map/all_gather | solution.py:639
  33.1 7.5 %copy-start.15 = (s32[896]{0:T(1024)}, s32[896]{0:T(1024)S(1)}, u32[]{:S(2)}) copy-start(s32[896]{0:T(1024)S(1)} %fusion.49) | copy-start | bytes 10756
  41.9 34.2 %all-to-all-start.2 = ((bf16[16,56,768]{2,1,0:T(8,128)(2,1)}), bf16[16,56,768]{2,1,0:T(8,128)(2,1)S(1)}, u32[]{:S(2)}, u32[]{:S(2)}) async-start(bf16[16,56,768]{2,1,0:T(8,128)(2,1)} %broadcast_select_fusion.3), calls=%async_computation.2 | async-start | bytes 2752512 | tf_op jit(solution)/shard_map/all_to_all | solution.py:679
  47.7 6.3 copy-start.11
  78.4 4.3 copy-start.12
  78.9 14.5 %copy-start.10 = (s32[32,568]{1,0:T(8,128)}, s32[32,568]{1,0:T(8,128)S(1)}, u32[]{:S(2)}) copy-start(s32[32,568]{1,0:T(8,128)S(1)} %get-tuple-element.487) | copy-start | bytes 218116
  78.9 42.4 %copy-start.2 = (bf16[512,768]{1,0:T(8,128)(2,1)}, bf16[512,768]{1,0:T(8,128)(2,1)S(1)}, u32[]{:S(2)}) copy-start(bf16[512,768]{1,0:T(8,128)(2,1)S(1)} %get-tuple-element.207) | copy-start | bytes 2359300
  93.4 36.4 %copy-start.13 = (f32[768]{0:T(1024)S(1)}, f32[768]{0:T(1024)}, u32[]{:S(2)}) copy-start(f32[768]{0:T(1024)} %param.19) | copy-start | bytes 9220
  128.6 1.1 copy-start.4
  384.6 2.4 copy-start.5
  384.6 2.8 copy-start.6
  387.4 10.3 %slice-start = ((s8[4718592]{0:T(1024)(128)(4,1)}), s8[4194304]{0:T(1024)(128)(4,1)S(1)}, s32[]{:S(2)}) async-start(s8[4718592]{0:T(1024)(128)(4,1)} %bitcast.91), calls=%async_computation.7 | async-start | bytes 8388608
  387.4 10.3 %slice-start.2 = ((s8[6291456]{0:T(1024)(128)(4,1)}), s8[4194304]{0:T(1024)(128)(4,1)S(1)}, s32[]{:S(2)}) async-start(s8[6291456]{0:T(1024)(128)(4,1)} %bitcast.93), calls=%async_computation.9 | async-start | bytes 8388608
  387.7 10.0 %slice-start.1 = ((s8[4718592]{0:T(1024)(128)(4,1)}), s8[524288]{0:T(1024)(128)(4,1)S(1)}, s32[]{:S(2)}) async-start(s8[4718592]{0:T(1024)(128)(4,1)} %bitcast.91), calls=%async_computation.8 | async-start | bytes 1048576
  387.7 10.0 %slice-start.3 = ((s8[6291456]{0:T(1024)(128)(4,1)}), s8[2097152]{0:T(1024)(128)(4,1)S(1)}, s32[]{:S(2)}) async-start(s8[6291456]{0:T(1024)(128)(4,1)} %bitcast.93), calls=%async_computation.10 | async-start | bytes 4194304
  397.7 5.0 copy-start.3
  421.1 0.7 copy-start.14
  421.8 4.0 copy-start
  421.8 4.0 copy-start.17
  429.3 200.2 %copy-start.16 = (pred[896]{0:T(1024)(128)(4,1)S(1)}, pred[896]{0:T(1024)(128)(4,1)}, u32[]{:S(2)}) copy-start(pred[896]{0:T(1024)(128)(4,1)} %lt.376) | copy-start | bytes 2692
  629.5 17.8 %copy-start.1 = (f32[512,768]{1,0:T(8,128)S(1)}, f32[512,768]{1,0:T(8,128)}, u32[]{:S(2)}) copy-start(f32[512,768]{1,0:T(8,128)} %copy-done) | copy-start | bytes 4718596
  648.0 8.3 %copy-start.9 = (f32[192,3072]{1,0:T(8,128)S(1)}, f32[192,3072]{1,0:T(8,128)}, u32[]{:S(2)}) copy-start(f32[192,3072]{1,0:T(8,128)} %get-tuple-element.473) | copy-start | bytes 7077892
  656.3 2.5 copy-start.8
  658.9 2.5 copy-start.7
Sparse Core Ops, SparseCore 0:
  16.3 5.7 sort.11.cloned.1.call-done
  (1 shorter events, 0.0 us)
Sparse Core Ops, SparseCore 1:
  19.5 63.1 all-gather.4
  84.8 36.5 all-gather.6
